TPU v7x, 32 devices: a whole 2x2x4 slice. The times are simulated.
32 devices in a mesh: gy: 8 (over z, x), gx: 4 (over y, core).
Axes of the slice: x: 2, y: 2, z: 4, core: 2. Of those that a mesh axis runs over, the one named last changes fastest.
Arguments:
- right_side: float32 [32, 512, 512], P(None, 'gy', 'gx'), may hold values from -32 to 32
- couplings: float32 [3, 512, 512], P(None, 'gy', 'gx'), may hold values from 0.1 to 0.5
- center: float32 [512, 512], P('gy', 'gx'), may hold values from 0.6 to 1.5
- ocean_mask: int32 [512, 512], P('gy', 'gx'), may hold values 0 or 1
Outputs:
- solution: float32 [32, 512, 512], P(None, 'gy', 'gx')
- residual: float32 [32, 512, 512], P(None, 'gy', 'gx')
All inputs are finite; a program needn't handle non-finite values. No bound on the sum of `ocean_mask` on one device may be relied on, other than what follows from the above.
Results may differ from a plain program's by a relative error of at most 0.0055.
Values sent between devices are 32-bit elements; how exact they have to be, the bound alone decides.
A program may use at most 64 MiB of HBM per device.

v0:
```python
import jax
import jax.numpy as jnp
from jax import lax
from jax.experimental import pallas as pl
from jax.experimental.pallas import tpu as pltpu
from jax.sharding import PartitionSpec as P

ITERS = 6
ROOT = 0.28
PAD = 16
VMEM = 67043328
GRANT = 24 * 1024 * 1024
PAIRS = [(i, j) for i in range(ITERS) for j in range(i, ITERS + 1)]
F32 = jnp.float32


def iota(dim):
    return lax.broadcasted_iota(jnp.int32, (8, 128), dim)


def along(x, idx, axis):
    return jnp.take_along_axis(x, idx, axis=axis, mode="promise_in_bounds")


def prepare(members, rows, top, planes, shifted, inv, links, square):
    groups = 128 // members
    sub_rows = rows // groups
    lanes = iota(1)
    group = lax.shift_right_logical(lanes, members.bit_length() - 1)
    seam = lanes == rows + 8
    folded = jnp.logical_and(top, lanes >= rows + 8)
    tiles = 18
    first = PAD - 8

    @pl.loop(0, tiles)
    def _(t):
        at = pl.ds(pl.multiple_of(first + 8 * t, 8), 8)
        nxt = pl.ds(first + 8 * t + 1, 8)
        for n, p in enumerate((1, 2)):
            shifted[n, at, :] = jnp.where(folded, planes[p, nxt, :], planes[p, at, :])

    def before(v):
        return pltpu.roll(v, 1, 1)

    def after(v):
        return pltpu.roll(v, 127, 1)

    @pl.loop(0, tiles)
    def _(t):
        at = pl.ds(pl.multiple_of(first + 8 * t, 8), 8)
        prv = pl.ds(first + 8 * t - 1, 8)
        cn, ce, cne = planes[0, at, :], shifted[0, at, :], shifted[1, at, :]
        cew, cnw = shifted[0, prv, :], shifted[1, prv, :]
        diag = planes[3, at, :] + cn + ce + cew + cne + cnw + before(cn + cne + cnw)
        ocean = planes[4, at, :] > 0.0
        root = jnp.sqrt(diag)
        recip = jnp.where(ocean, 1.0 / root, 0.0)
        root = jnp.where(ocean, root, 0.0)
        inv[at, :] = jnp.where(seam, after(recip), recip)
        square[at, :] = root

    @pl.loop(0, tiles)
    def _(t):
        at = pl.ds(pl.multiple_of(first + 8 * t, 8), 8)
        nxt = pl.ds(first + 8 * t + 1, 8)
        here, east = inv[at, :], inv[nxt, :]
        up, up_east = after(here), after(east)
        here_up = jnp.where(seam, before(here), here)
        east_up = jnp.where(seam, before(east), east)
        factor = 1.0 / ROOT
        cn, ce, cne = planes[0, at, :] * factor, shifted[0, at, :] * factor, shifted[1, at, :] * factor
        values = (cn * here_up * up, ce * here * east, cne * here_up * up_east, cne * east_up * up)
        step = group * sub_rows
        extra = (group == groups - 1).astype(jnp.int32)
        count = sub_rows + 2 * ITERS
        for r in range(count + 1):
            if r < sub_rows + ITERS:
                idx = step + (r + 8 - ITERS)
            else:
                idx = step + extra + (r + 7 - ITERS)
            for n, v in enumerate(values):
                links[n, r, at, :] = along(v, idx, 1)


def iterate(members, rows, raw, inv, links, basis, gram_ref):
    groups = 128 // members
    sub_rows = rows // groups
    lanes, subs = iota(1), iota(0)
    group = lax.shift_right_logical(lanes, members.bit_length() - 1)
    step = group * sub_rows
    extra = (group == groups - 1).astype(jnp.int32)

    @pl.loop(0, 18)
    def _(t):
        at = pl.ds(pl.multiple_of(PAD - 8 + 8 * t, 8), 8)
        here = inv[at, :]
        for r in range(sub_rows + 2 * ITERS):
            if r < sub_rows + ITERS:
                idx = step + (r + 8 - ITERS)
            else:
                idx = step + extra + (r + 8 - ITERS)
            basis[0][r, at, :] = raw[r, at, :] * along(here, idx, 1)

    for k in range(ITERS):
        depth = ITERS - 1 - k
        here, out = basis[k], basis[k + 1]
        old = basis[k - 1] if k else None

        @pl.loop(0, (128 + 2 * depth + 7) // 8)
        def _(t):
            x0 = PAD - depth + 8 * t
            mid, east, west = pl.ds(x0, 8), pl.ds(x0 + 1, 8), pl.ds(x0 - 1, 8)

            def three(r):
                return here[r, west, :], here[r, mid, :], here[r, east, :]

            start, stop = ITERS - depth, ITERS + sub_rows + depth
            dn, cur = three(start - 1), three(start)
            north = links[0, start - 1, mid, :]
            for r in range(start, stop):
                nxt = three(r + 1)
                c = r + (1 if r >= ITERS + sub_rows else 0)
                if r == ITERS + sub_rows:
                    north = links[0, c - 1, mid, :]
                south, north = north, links[0, c, mid, :]
                total = (north * nxt[1] + south * dn[1]) + (
                    links[1, c, mid, :] * cur[2] + links[1, c, west, :] * cur[0]
                )
                total = total + (links[2, c, mid, :] * nxt[2] + links[2, c - 1, west, :] * dn[0])
                total = total + (links[3, c, west, :] * nxt[0] + links[3, c - 1, mid, :] * dn[2])
                if old is not None:
                    total = total - old[r, mid, :]
                out[r, mid, :] = total
                dn, cur = cur, nxt

    def body(r, sums):
        sums = list(sums)
        for t in range(16):
            at = slice(PAD + 8 * t, PAD + 8 * t + 8)
            vs = [basis[k][r + ITERS, at, :] for k in range(ITERS + 1)]
            for n, (i, j) in enumerate(PAIRS):
                sums[n] = sums[n] + vs[i] * vs[j]
        return tuple(sums)

    zero = jnp.zeros((8, 128), F32)
    sums = lax.fori_loop(0, sub_rows, body, (zero,) * len(PAIRS))
    pack = [zero] * 4
    for n, s in enumerate(sums):
        for step in (1, 2, 4):
            s = s + pltpu.roll(s, step, 0)
        pack[n // 8] = jnp.where(subs == n % 8, s, pack[n // 8])
    total = zero
    for j, v in enumerate(pack):
        width = members
        while width < 128:
            v = v + pltpu.roll(v, width, 1)
            width *= 2
        total = jnp.where(group == j, v, total)
    gram_ref[...] = total


def coefficients(gram):
    def g(i, j):
        return gram[min(i, j)][max(i, j)]

    def applied(p):
        q = []
        for k in range(ITERS + 1):
            terms = []
            if k < len(p):
                terms.append(p[k])
            if 0 < k <= len(p):
                terms.append(-ROOT * p[k - 1])
            if k + 1 < len(p):
                terms.append(-ROOT * p[k + 1])
            if terms:
                q.append(sum(terms[1:], terms[0]))
        return q

    def inner(p, q):
        total = None
        for i, a in enumerate(p):
            row = None
            for j, b in enumerate(q):
                t = g(i, j) * b
                row = t if row is None else row + t
            t = a * row
            total = t if total is None else total + t
        return total

    one = jnp.ones_like(gram[0][0])
    z, p, x = [one], [one], []
    rz = g(0, 0)
    for iteration in range(ITERS):
        q = applied(p)
        step = rz / inner(p, q)
        x = [(x[k] if k < len(x) else 0.0) + step * p[k] for k in range(len(p))]
        z = [(z[k] if k < len(z) else 0.0) - step * q[k] for k in range(len(q))]
        if iteration + 1 < ITERS:
            rz_new = inner(z, z)
            beta = rz_new / rz
            p = [z[k] + (beta * p[k] if k < len(p) else 0.0) for k in range(len(z))]
            rz = rz_new
    return x, z


def combine(members, rows, basis, scale_ref, sums, outs, stage, sems):
    groups = 128 // members
    sub_rows = rows // groups
    tall = stage.shape[2]
    lanes = iota(1)
    tiles = [along(sums, (lanes & (members - 1)) + members * j, 1) for j in range(4)]
    gram = [[None] * (ITERS + 1) for _ in range(ITERS + 1)]
    for n, (i, j) in enumerate(PAIRS):
        gram[i][j] = jnp.broadcast_to(tiles[n // 8][n % 8 : n % 8 + 1, :], (8, 128))
    xs, zs = coefficients(gram)
    flat = stage.reshape(2 * members * tall, 128)
    blocks = members // 8
    half = sub_rows // 2

    def drain(h):
        copies = []
        for o in range(2):
            for g in range(groups):
                at = slice(sub_rows * g + half * h, sub_rows * g + half * (h + 1))
                copies.append(
                    pltpu.make_async_copy(stage.at[o, :, at, :], outs[o].at[:, at, :], sems.at[h, o, g])
                )
        return copies

    started = []
    for h in range(2):

        @pl.loop(half * h, half * (h + 1))
        def _(r):
            found = ([], [])
            for t in range(16):
                at = slice(PAD + 8 * t, PAD + 8 * t + 8)
                vs = [basis[k][r + ITERS, at, :] for k in range(ITERS + 1)]
                found[0].append(sum((xs[k] * vs[k] for k in range(1, ITERS)), xs[0] * vs[0]))
                found[1].append(sum((zs[k] * vs[k] for k in range(1, ITERS + 1)), zs[0] * vs[0]))
            for o in range(2):
                turned = jnp.concatenate(found[o], axis=0).T
                for g in range(groups):
                    row = sub_rows * g + r
                    scale = jnp.broadcast_to(scale_ref[o, pl.ds(row + 8, 1), :], (8, 128))
                    for b in range(blocks):
                        n = 8 * (g * blocks + b)
                        at = pl.ds((o * members + 8 * b) * tall + row, 8, stride=tall)
                        flat[at, :] = turned[n : n + 8, :] * scale

        for c in drain(h):
            c.start()
            started.append(c)
    for c in started:
        c.wait()


def solve_kernel(members, rows, ny, nx, rhs_hbm, coup_hbm, center_hbm, mask_hbm, *refs):
    outs, basis = refs[:2], refs[2 : ITERS + 3]
    (
        scale_ref, stage, drain, field, planes, rhs, coup, center, mask, coef_out, coef_in, rows_out, rows_in, ext,
        shifted, inv, links, square, gram, along_x, along_y, load, send, recv,
    ) = refs[ITERS + 3 :]
    groups = 128 // members
    sub_rows = rows // groups
    tall = rhs.shape[1]
    y, x = lax.axis_index("gy"), lax.axis_index("gx")
    top = (y + 1) // ny
    mirror = nx - 1 - x
    east, west = lax.rem(x + 1, nx), lax.rem(x + nx - 1, nx)
    up = (y + 1 - top, x + top * (mirror - x))
    down = (jnp.maximum(y - 1, 0), x)
    loads = [
        pltpu.make_async_copy(coup_hbm, coup, load.at[0]),
        pltpu.make_async_copy(center_hbm, center, load.at[1]),
        pltpu.make_async_copy(mask_hbm, mask, load.at[2]),
        pltpu.make_async_copy(rhs_hbm, rhs.at[:, 0:rows, :], load.at[3]),
    ]
    for c in loads:
        c.start()
    barrier = pltpu.get_barrier_semaphore()

    def greet(there):
        pl.semaphore_signal(barrier, inc=1, device_id=there, device_id_type=pl.DeviceIdType.MESH)

    for step in range(1, nx):
        greet((y, lax.rem(x + step, nx)))
    for step in range(1, ny):
        greet((lax.rem(y + step, ny), x))

    def copy(src, dst, n, m, there):
        return pltpu.make_async_remote_copy(
            src_ref=src,
            dst_ref=dst,
            send_sem=send.at[n],
            recv_sem=recv.at[m],
            device_id=there,
            device_id_type=pl.DeviceIdType.MESH,
        )

    lanes, subs = iota(1), iota(0)
    flip_lane = jnp.where(top == 1, 127 - lanes, lanes)
    flip_sub = jnp.where(top == 1, 7 - subs, subs)
    for c in loads[:3]:
        c.wait()

    def own(p, at):
        if p < 3:
            return coup[p, at, :]
        return center[at, :] if p == 3 else mask[at, :].astype(F32)

    for p in range(5):
        coef_out[0, p] = along(along(own(p, slice(rows - 8, rows)), flip_lane, 1), flip_sub, 0)
        coef_out[1, p] = own(p, slice(0, 8))
    pl.semaphore_wait(barrier, nx + ny - 2)

    coef_up = copy(coef_out.at[0], coef_in.at[top], 0, top, up)
    coef_down = copy(coef_out.at[1], coef_in.at[1], 1, 1, down)
    rows_up = copy(rows_out.at[0], rows_in.at[top], 2, 2 + top, up)
    rows_down = copy(rows_out.at[1], rows_in.at[1], 3, 3, down)
    coef_up.start()

    @pl.when(y > 0)
    def _():
        coef_down.start()

    flat = rhs.reshape(members * tall, 128)

    def column(row, block):
        return flat[pl.ds(8 * block * tall + row, 8, stride=tall), :]

    blocks = members // 8
    loads[3].wait()
    for q in range(ITERS):
        high = rows - ITERS + q + top * (ITERS - 1 - 2 * q)
        for b in range(blocks):
            at = slice(q * members + 8 * b, q * members + 8 * b + 8)
            rows_out[0, at, :] = along(column(high, b), flip_lane, 1)
            rows_out[1, at, :] = column(q, b)
    rows_up.start()

    @pl.when(y > 0)
    def _():
        rows_down.start()

    @pl.loop(0, sub_rows)
    def _(r):
        stack = [column(sub_rows * g + r, b) for g in range(groups) for b in range(blocks)]
        field[r + ITERS, PAD : PAD + 128, :] = jnp.concatenate(stack, axis=0).T

    coef_north = copy(coef_out.at[1], coef_in.at[1], 1, 1, down)
    coef_south = copy(coef_out.at[0], coef_in.at[0], 0, 0, up)
    coef_north.wait_recv()

    @pl.when(y > 0)
    def _():
        coef_south.wait_recv()

    for p in range(5):
        beyond = coef_in[1, p]
        moved = pltpu.roll(beyond, 1, 0)
        if p in (0, 2):
            last = jnp.broadcast_to(own(p, slice(rows - 1, rows)), (8, 128))
            beyond = jnp.where(top == 1, beyond, jnp.where(subs == 0, last, moved))
        else:
            beyond = jnp.where(subs == 0, beyond, moved)
        ext[0:8, :] = jnp.where(y == 0, 0.0, coef_in[0, p])
        ext[8 : rows + 8, :] = own(p, slice(0, rows))
        ext[rows + 8 : rows + 16, :] = beyond
        ext[rows + 16 : 128, :] = jnp.zeros((112 - rows, 128), F32)
        planes[p, PAD : PAD + 128, :] = ext[...].T

    def sideways(ref, n):
        return [
            copy(ref.at[:, PAD : PAD + 8, :], ref.at[:, PAD + 128 : PAD + 136, :], n, n, (y, west)),
            copy(ref.at[:, PAD + 120 : PAD + 128, :], ref.at[:, PAD - 8 : PAD, :], n + 1, n + 1, (y, east)),
        ]

    sides = sideways(planes, 4)
    for c in sides:
        c.start()
    for c in sides:
        c.wait()
    prepare(members, rows, y == ny - 1, planes, shifted, inv, links, square)
    copy(rows_out.at[1], rows_in.at[1], 3, 3, down).wait_recv()

    @pl.when(y > 0)
    def _():
        copy(rows_out.at[0], rows_in.at[0], 2, 2, up).wait_recv()

    @pl.loop(0, ITERS)
    def _(q):
        def arrived(side, b):
            return rows_in[side, pl.ds(pl.multiple_of(q * members, 8) + 8 * b, 8), :]

        low = [jnp.where(y == 0, 0.0, arrived(0, b)) for b in range(blocks)]
        low += [column(sub_rows * g - ITERS + q, b) for g in range(1, groups) for b in range(blocks)]
        field[q, PAD : PAD + 128, :] = jnp.concatenate(low, axis=0).T
        high = [column(sub_rows * g + q, b) for g in range(1, groups) for b in range(blocks)]
        high += [arrived(1, b) for b in range(blocks)]
        field[q + ITERS + sub_rows, PAD : PAD + 128, :] = jnp.concatenate(high, axis=0).T

    more = sideways(field, 6)
    for c in more:
        c.start()
    coef_up.wait_send()
    rows_up.wait_send()

    @pl.when(y > 0)
    def _():
        coef_down.wait_send()
        rows_down.wait_send()

    for c in more:
        c.wait()
    iterate(members, rows, field, inv, links, basis, gram)

    def sent(source, dst, n, there):
        c = copy(source, dst, n, n, there)
        c.start()
        return c

    across = [sent(gram, along_x.at[s], 7 + s, (y, lax.rem(x + s, nx))) for s in range(1, nx)]
    scale_ref[0] = inv[PAD : PAD + 128, :].T
    scale_ref[1] = square[PAD : PAD + 128, :].T
    for c in across:
        c.wait()
    along_x[0] = sum((along_x[s] for s in range(1, nx)), gram[...])
    across = [
        sent(along_x.at[0], along_y.at[s], 6 + nx + s, (lax.rem(y + s, ny), x)) for s in range(1, ny)
    ]
    for c in across:
        c.wait()
    sums = sum((along_y[s] for s in range(1, ny)), along_x[0])
    combine(members, rows, basis, scale_ref, sums, outs, stage, drain)


def on_device(right_side, couplings, center, ocean_mask):
    members, rows, columns = right_side.shape
    groups = 128 // members
    sub_rows = rows // groups
    assert columns == 128 and members % 8 == 0 and groups * members == 128
    assert rows <= 104 and sub_rows % 16 == 0 and sub_rows >= ITERS
    ny, nx = lax.axis_size("gy"), lax.axis_size("gx")
    vmem = pl.BlockSpec(memory_space=pltpu.VMEM)
    hbm = pl.BlockSpec(memory_space=pltpu.HBM)
    deep, wide = sub_rows + 2 * ITERS, columns + 2 * PAD + 8

    kernel_vmem = 60 * 1024 * 1024

    def first(*refs):
        solve_kernel(members, rows, ny, nx, *refs)

    return pl.pallas_call(
        first,
        out_shape=(jax.ShapeDtypeStruct(right_side.shape, F32),) * 2,
        in_specs=[hbm] * 4,
        out_specs=(hbm, hbm),
        scratch_shapes=[pltpu.VMEM((deep, wide, 128), F32)] * (ITERS + 1)
        + [
            pltpu.VMEM((2, 128, 128), F32),
            pltpu.VMEM((2, members, rows + 8, columns), F32),
            pltpu.SemaphoreType.DMA((2, 2, groups)),
            pltpu.VMEM((deep, wide, 128), F32),
            pltpu.VMEM((5, wide, 128), F32),
            pltpu.VMEM((members, rows + 8, columns), F32),
            pltpu.VMEM((3, rows, columns), F32),
            pltpu.VMEM((rows, columns), F32),
            pltpu.VMEM((rows, columns), jnp.int32),
            pltpu.VMEM((2, 5, 8, columns), F32),
            pltpu.VMEM((2, 5, 8, columns), F32),
            pltpu.VMEM((2, ITERS * members, columns), F32),
            pltpu.VMEM((2, ITERS * members, columns), F32),
            pltpu.VMEM((128, 128), F32),
            pltpu.VMEM((2, wide, 128), F32),
            pltpu.VMEM((wide, 128), F32),
            pltpu.VMEM((4, deep + 1, wide, 128), F32),
            pltpu.VMEM((wide, 128), F32),
            pltpu.VMEM((8, 128), F32),
            pltpu.VMEM((nx, 8, 128), F32),
            pltpu.VMEM((ny, 8, 128), F32),
            pltpu.SemaphoreType.DMA((4,)),
            pltpu.SemaphoreType.DMA((6 + nx + ny,)),
            pltpu.SemaphoreType.DMA((6 + nx + ny,)),
        ],
        compiler_params=pltpu.CompilerParams(
            collective_id=0, has_side_effects=True, vmem_limit_bytes=kernel_vmem
        ),
    )(right_side, couplings, center, ocean_mask)


def solution(mesh):
    in_specs = (P(None, "gy", "gx"), P(None, "gy", "gx"), P("gy", "gx"), P("gy", "gx"))
    out_specs = (P(None, "gy", "gx"), P(None, "gy", "gx"))
    return jax.shard_map(
        on_device, mesh=mesh, in_specs=in_specs, out_specs=out_specs, check_vma=False
    )
```

profile of v0, /device:TPU:0, one launch (start us, length us, event | category | flops | bytes accessed | tf_op | source)
XLA Modules:
  0.0 50.9 jit_solution(7563293324889464478)
XLA Ops:
  0.6 46.9 %shard_map.59 = (f32[32,64,128]{2,1,0:T(8,128)}, f32[32,64,128]{2,1,0:T(8,128)}) custom-call(f32[32,64,128]{2,1,0:T(8,128)} %refs_0_.1, f32[3,64,128]{2,1,0:T(8,128)} %refs_1_.1, f32[64,128]{1,0:T(8,128)} %refs_2_.1, s32[64,128]{1,0:T(8,128)} %refs_3_.1), custom_call_target="tpu_custom_call" | custom-call | tf_op jit(solution)/shard_map/pallas_call | solution.py:455
  47.5 0.0 copy-start
  47.5 2.4 %copy.8 = f32[32,64,128]{2,1,0:T(8,128)} copy(f32[32,64,128]{2,1,0:T(8,128)} %get-tuple-element.4) | data formatting | bytes 2097152
  49.9 0.0 copy-done
  49.9 1.0 %copy.9 = f32[32,64,128]{2,1,0:T(8,128)} copy(f32[32,64,128]{2,1,0:T(8,128)S(1)} %copy-done) | data formatting | bytes 2097152
Async XLA Ops:
  47.5 2.4 %copy-start = (f32[32,64,128]{2,1,0:T(8,128)S(1)}, f32[32,64,128]{2,1,0:T(8,128)}, u32[]{:S(2)}) copy-start(f32[32,64,128]{2,1,0:T(8,128)} %get-tuple-element.5) | copy-start | bytes 3145732
where the time goes:
time: 51 us; the launch traced here: 50.9 us
  Pallas kernels  46.9 us (92%)
  local copies, waits for them, and re-layouts  3.37 us (7%)
  between operations  0.65 us (1%)
    pallas_call x1, Pallas kernels, on_device(): pl.pallas_call(first, out_shape=(jax.ShapeDtypeStruct(right_side.shape, F...  46.9 us
    unnamed x4, local copies, waits for them, and re-layouts  3.37 us

commit v1 on v0

--- a/solution.py
+++ b/solution.py
@@ -22,11 +22,8 @@
     return jnp.take_along_axis(x, idx, axis=axis, mode="promise_in_bounds")
 
 
-def prepare(members, rows, top, planes, shifted, inv, links, square):
-    groups = 128 // members
-    sub_rows = rows // groups
+def prepare(members, rows, top, planes, shifted, inv, links, square, lhs, pick):
     lanes = iota(1)
-    group = lax.shift_right_logical(lanes, members.bit_length() - 1)
     seam = lanes == rows + 8
     folded = jnp.logical_and(top, lanes >= rows + 8)
     tiles = 18
@@ -59,27 +56,61 @@
         inv[at, :] = jnp.where(seam, after(recip), recip)
         square[at, :] = root
 
-    @pl.loop(0, tiles)
+    span = rows + 16
+    lanes = lax.broadcasted_iota(jnp.int32, (16, 128), 1)
+    seam = lanes == rows + 8
+
+    @pl.loop(0, tiles // 2)
     def _(t):
-        at = pl.ds(pl.multiple_of(first + 8 * t, 8), 8)
-        nxt = pl.ds(first + 8 * t + 1, 8)
+        at = pl.ds(pl.multiple_of(first + 16 * t, 8), 16)
+        nxt = pl.ds(first + 16 * t + 1, 16)
         here, east = inv[at, :], inv[nxt, :]
         up, up_east = after(here), after(east)
         here_up = jnp.where(seam, before(here), here)
         east_up = jnp.where(seam, before(east), east)
         factor = 1.0 / ROOT
         cn, ce, cne = planes[0, at, :] * factor, shifted[0, at, :] * factor, shifted[1, at, :] * factor
-        values = (cn * here_up * up, ce * here * east, cne * here_up * up_east, cne * east_up * up)
-        step = group * sub_rows
-        extra = (group == groups - 1).astype(jnp.int32)
-        count = sub_rows + 2 * ITERS
-        for r in range(count + 1):
-            if r < sub_rows + ITERS:
-                idx = step + (r + 8 - ITERS)
-            else:
-                idx = step + extra + (r + 7 - ITERS)
-            for n, v in enumerate(values):
-                links[n, r, at, :] = along(v, idx, 1)
+        values = (cn * here_up * up, ce * here * east, cne * here_up * up_east, cne * east_up * up, here)
+        for n, v in enumerate(values):
+            top_part = v.astype(jnp.bfloat16).astype(F32)
+            v = v - top_part
+            mid_part = v.astype(jnp.bfloat16).astype(F32)
+            moved = pltpu.roll(mid_part, span, 1)
+            low_part = pltpu.roll(v - mid_part, 2 * span - 128, 1)
+            left = jnp.where(lanes < span, top_part, moved)
+            right = jnp.where(lanes < 2 * span - 128, moved, low_part)
+            right = jnp.where(lanes < 3 * span - 128, right, 0.0)
+            to = pl.ds(pl.multiple_of(8 * tiles * n + 16 * t, 16), 16)
+            lhs[to, 0:128] = left.astype(jnp.bfloat16)
+            lhs[to, 128:256] = right.astype(jnp.bfloat16)
+
+    @pl.loop(0, links.shape[1] // 2)
+    def _(p):
+        found = jnp.dot(lhs[...], pick[p], preferred_element_type=F32)
+        for n in range(5):
+            for h in range(2):
+                links[n, 2 * p + h, first : first + 8 * tiles, :] = found[
+                    8 * tiles * n : 8 * tiles * (n + 1), 128 * h : 128 * h + 128
+                ]
+
+
+def choose(members, rows, pick):
+    groups = 128 // members
+    sub_rows = rows // groups
+    span = rows + 16
+    source = lax.broadcasted_iota(jnp.int32, (256, 256), 0)
+    lane = lax.broadcasted_iota(jnp.int32, (256, 256), 1)
+    source = source - span * ((source >= span).astype(jnp.int32) + (source >= 2 * span).astype(jnp.int32))
+    group = lax.shift_right_logical(lane & 127, members.bit_length() - 1)
+    half = lax.shift_right_logical(lane, 7)
+    last = (group == groups - 1).astype(jnp.int32)
+    base = source - sub_rows * group - half - 8 + ITERS
+
+    @pl.loop(0, pick.shape[0])
+    def _(p):
+        later = (2 * p + half >= sub_rows + ITERS).astype(jnp.int32)
+        hit = base == 2 * p + later * (last - 1)
+        pick[p] = jnp.where(hit, 1.0, 0.0).astype(jnp.bfloat16)
 
 
 def iterate(members, rows, raw, inv, links, basis, gram_ref):
@@ -87,19 +118,13 @@
     sub_rows = rows // groups
     lanes, subs = iota(1), iota(0)
     group = lax.shift_right_logical(lanes, members.bit_length() - 1)
-    step = group * sub_rows
-    extra = (group == groups - 1).astype(jnp.int32)
-
-    @pl.loop(0, 18)
-    def _(t):
-        at = pl.ds(pl.multiple_of(PAD - 8 + 8 * t, 8), 8)
-        here = inv[at, :]
-        for r in range(sub_rows + 2 * ITERS):
-            if r < sub_rows + ITERS:
-                idx = step + (r + 8 - ITERS)
-            else:
-                idx = step + extra + (r + 8 - ITERS)
-            basis[0][r, at, :] = raw[r, at, :] * along(here, idx, 1)
+
+    @pl.loop(0, sub_rows + 2 * ITERS)
+    def _(r):
+        c = r + (r >= sub_rows + ITERS).astype(jnp.int32)
+        for t in range(18):
+            at = slice(PAD - 8 + 8 * t, PAD + 8 * t)
+            basis[0][r, at, :] = raw[r, at, :] * links[4, c, at, :]
 
     for k in range(ITERS):
         depth = ITERS - 1 - k
@@ -159,108 +184,11 @@
     gram_ref[...] = total
 
 
-def coefficients(gram):
-    def g(i, j):
-        return gram[min(i, j)][max(i, j)]
-
-    def applied(p):
-        q = []
-        for k in range(ITERS + 1):
-            terms = []
-            if k < len(p):
-                terms.append(p[k])
-            if 0 < k <= len(p):
-                terms.append(-ROOT * p[k - 1])
-            if k + 1 < len(p):
-                terms.append(-ROOT * p[k + 1])
-            if terms:
-                q.append(sum(terms[1:], terms[0]))
-        return q
-
-    def inner(p, q):
-        total = None
-        for i, a in enumerate(p):
-            row = None
-            for j, b in enumerate(q):
-                t = g(i, j) * b
-                row = t if row is None else row + t
-            t = a * row
-            total = t if total is None else total + t
-        return total
-
-    one = jnp.ones_like(gram[0][0])
-    z, p, x = [one], [one], []
-    rz = g(0, 0)
-    for iteration in range(ITERS):
-        q = applied(p)
-        step = rz / inner(p, q)
-        x = [(x[k] if k < len(x) else 0.0) + step * p[k] for k in range(len(p))]
-        z = [(z[k] if k < len(z) else 0.0) - step * q[k] for k in range(len(q))]
-        if iteration + 1 < ITERS:
-            rz_new = inner(z, z)
-            beta = rz_new / rz
-            p = [z[k] + (beta * p[k] if k < len(p) else 0.0) for k in range(len(z))]
-            rz = rz_new
-    return x, z
-
-
-def combine(members, rows, basis, scale_ref, sums, outs, stage, sems):
-    groups = 128 // members
-    sub_rows = rows // groups
-    tall = stage.shape[2]
-    lanes = iota(1)
-    tiles = [along(sums, (lanes & (members - 1)) + members * j, 1) for j in range(4)]
-    gram = [[None] * (ITERS + 1) for _ in range(ITERS + 1)]
-    for n, (i, j) in enumerate(PAIRS):
-        gram[i][j] = jnp.broadcast_to(tiles[n // 8][n % 8 : n % 8 + 1, :], (8, 128))
-    xs, zs = coefficients(gram)
-    flat = stage.reshape(2 * members * tall, 128)
-    blocks = members // 8
-    half = sub_rows // 2
-
-    def drain(h):
-        copies = []
-        for o in range(2):
-            for g in range(groups):
-                at = slice(sub_rows * g + half * h, sub_rows * g + half * (h + 1))
-                copies.append(
-                    pltpu.make_async_copy(stage.at[o, :, at, :], outs[o].at[:, at, :], sems.at[h, o, g])
-                )
-        return copies
-
-    started = []
-    for h in range(2):
-
-        @pl.loop(half * h, half * (h + 1))
-        def _(r):
-            found = ([], [])
-            for t in range(16):
-                at = slice(PAD + 8 * t, PAD + 8 * t + 8)
-                vs = [basis[k][r + ITERS, at, :] for k in range(ITERS + 1)]
-                found[0].append(sum((xs[k] * vs[k] for k in range(1, ITERS)), xs[0] * vs[0]))
-                found[1].append(sum((zs[k] * vs[k] for k in range(1, ITERS + 1)), zs[0] * vs[0]))
-            for o in range(2):
-                turned = jnp.concatenate(found[o], axis=0).T
-                for g in range(groups):
-                    row = sub_rows * g + r
-                    scale = jnp.broadcast_to(scale_ref[o, pl.ds(row + 8, 1), :], (8, 128))
-                    for b in range(blocks):
-                        n = 8 * (g * blocks + b)
-                        at = pl.ds((o * members + 8 * b) * tall + row, 8, stride=tall)
-                        flat[at, :] = turned[n : n + 8, :] * scale
-
-        for c in drain(h):
-            c.start()
-            started.append(c)
-    for c in started:
-        c.wait()
-
-
 def solve_kernel(members, rows, ny, nx, rhs_hbm, coup_hbm, center_hbm, mask_hbm, *refs):
-    outs, basis = refs[:2], refs[2 : ITERS + 3]
+    basis, (scale_ref, sum_ref) = refs[: ITERS + 1], refs[ITERS + 1 : ITERS + 3]
     (
-        scale_ref, stage, drain, field, planes, rhs, coup, center, mask, coef_out, coef_in, rows_out, rows_in, ext,
-        shifted, inv, links, square, gram, along_x, along_y, load, send, recv,
+        field, planes, rhs, coup, center, mask, coef_out, coef_in, rows_out, rows_in, ext,
+        shifted, inv, links, square, lhs, pick, gram, along_x, along_y, load, send, recv,
     ) = refs[ITERS + 3 :]
     groups = 128 // members
     sub_rows = rows // groups
@@ -313,6 +241,7 @@
     for p in range(5):
         coef_out[0, p] = along(along(own(p, slice(rows - 8, rows)), flip_lane, 1), flip_sub, 0)
         coef_out[1, p] = own(p, slice(0, 8))
+    choose(members, rows, pick)
     pl.semaphore_wait(barrier, nx + ny - 2)
 
     coef_up = copy(coef_out.at[0], coef_in.at[top], 0, top, up)
@@ -380,9 +309,6 @@
     sides = sideways(planes, 4)
     for c in sides:
         c.start()
-    for c in sides:
-        c.wait()
-    prepare(members, rows, y == ny - 1, planes, shifted, inv, links, square)
     copy(rows_out.at[1], rows_in.at[1], 3, 3, down).wait_recv()
 
     @pl.when(y > 0)
@@ -412,6 +338,9 @@
         coef_down.wait_send()
         rows_down.wait_send()
 
+    for c in sides:
+        c.wait()
+    prepare(members, rows, y == ny - 1, planes, shifted, inv, links, square, lhs, pick)
     for c in more:
         c.wait()
     iterate(members, rows, field, inv, links, basis, gram)
@@ -432,8 +361,107 @@
     ]
     for c in across:
         c.wait()
-    sums = sum((along_y[s] for s in range(1, ny)), along_x[0])
-    combine(members, rows, basis, scale_ref, sums, outs, stage, drain)
+    sum_ref[...] = sum((along_y[s] for s in range(1, ny)), along_x[0])
+
+
+def coefficients(gram):
+    def g(i, j):
+        return gram[min(i, j)][max(i, j)]
+
+    def applied(p):
+        q = []
+        for k in range(ITERS + 1):
+            terms = []
+            if k < len(p):
+                terms.append(p[k])
+            if 0 < k <= len(p):
+                terms.append(-ROOT * p[k - 1])
+            if k + 1 < len(p):
+                terms.append(-ROOT * p[k + 1])
+            if terms:
+                q.append(sum(terms[1:], terms[0]))
+        return q
+
+    def inner(p, q):
+        total = None
+        for i, a in enumerate(p):
+            row = None
+            for j, b in enumerate(q):
+                t = g(i, j) * b
+                row = t if row is None else row + t
+            t = a * row
+            total = t if total is None else total + t
+        return total
+
+    one = jnp.ones_like(gram[0][0])
+    z, p, x = [one], [one], []
+    rz = g(0, 0)
+    for iteration in range(ITERS):
+        q = applied(p)
+        step = rz / inner(p, q)
+        x = [(x[k] if k < len(x) else 0.0) + step * p[k] for k in range(len(p))]
+        z = [(z[k] if k < len(z) else 0.0) - step * q[k] for k in range(len(q))]
+        if iteration + 1 < ITERS:
+            rz_new = inner(z, z)
+            beta = rz_new / rz
+            p = [z[k] + (beta * p[k] if k < len(p) else 0.0) for k in range(len(z))]
+            rz = rz_new
+    return x, z
+
+
+def combine_kernel(members, rows, *refs):
+    basis, (scale_ref, sum_ref, x_out, r_out, stage, sems) = refs[: ITERS + 1], refs[ITERS + 1 :]
+    groups = 128 // members
+    sub_rows = rows // groups
+    tall = stage.shape[2]
+    lanes = iota(1)
+    sums = sum_ref[...]
+    tiles = [along(sums, (lanes & (members - 1)) + members * j, 1) for j in range(4)]
+    gram = [[None] * (ITERS + 1) for _ in range(ITERS + 1)]
+    for n, (i, j) in enumerate(PAIRS):
+        gram[i][j] = jnp.broadcast_to(tiles[n // 8][n % 8 : n % 8 + 1, :], (8, 128))
+    xs, zs = coefficients(gram)
+    flat = stage.reshape(2 * members * tall, 128)
+    blocks = members // 8
+    half = sub_rows // 2
+    outs = (x_out, r_out)
+
+    def drain(h):
+        copies = []
+        for o in range(2):
+            for g in range(groups):
+                at = slice(sub_rows * g + half * h, sub_rows * g + half * (h + 1))
+                copies.append(
+                    pltpu.make_async_copy(stage.at[o, :, at, :], outs[o].at[:, at, :], sems.at[h, o, g])
+                )
+        return copies
+
+    started = []
+    for h in range(2):
+
+        @pl.loop(half * h, half * (h + 1))
+        def _(r):
+            found = ([], [])
+            for t in range(16):
+                at = slice(PAD + 8 * t, PAD + 8 * t + 8)
+                vs = [basis[k][r + ITERS, at, :] for k in range(ITERS + 1)]
+                found[0].append(sum((xs[k] * vs[k] for k in range(1, ITERS)), xs[0] * vs[0]))
+                found[1].append(sum((zs[k] * vs[k] for k in range(1, ITERS + 1)), zs[0] * vs[0]))
+            for o in range(2):
+                turned = jnp.concatenate(found[o], axis=0).T
+                for g in range(groups):
+                    row = sub_rows * g + r
+                    scale = jnp.broadcast_to(scale_ref[o, pl.ds(row + 8, 1), :], (8, 128))
+                    for b in range(blocks):
+                        n = 8 * (g * blocks + b)
+                        at = pl.ds((o * members + 8 * b) * tall + row, 8, stride=tall)
+                        flat[at, :] = turned[n : n + 8, :] * scale
+
+        for c in drain(h):
+            c.start()
+            started.append(c)
+    for c in started:
+        c.wait()
 
 
 def on_device(right_side, couplings, center, ocean_mask):
@@ -441,27 +469,27 @@
     groups = 128 // members
     sub_rows = rows // groups
     assert columns == 128 and members % 8 == 0 and groups * members == 128
-    assert rows <= 104 and sub_rows % 16 == 0 and sub_rows >= ITERS
+    assert 3 * (rows + 16) <= 256 < 4 * (rows + 16) and 2 * (rows + 16) >= 128 and sub_rows % 16 == 0 and sub_rows >= ITERS
     ny, nx = lax.axis_size("gy"), lax.axis_size("gx")
     vmem = pl.BlockSpec(memory_space=pltpu.VMEM)
     hbm = pl.BlockSpec(memory_space=pltpu.HBM)
     deep, wide = sub_rows + 2 * ITERS, columns + 2 * PAD + 8
 
-    kernel_vmem = 60 * 1024 * 1024
+    inputs = [
+        pltpu.with_memory_space_constraint(v, pltpu.HBM)
+        for v in (right_side, couplings, center, ocean_mask)
+    ]
 
     def first(*refs):
         solve_kernel(members, rows, ny, nx, *refs)
 
-    return pl.pallas_call(
+    *basis, scale, sums = pl.pallas_call(
         first,
-        out_shape=(jax.ShapeDtypeStruct(right_side.shape, F32),) * 2,
+        out_shape=(pltpu.VMEM((deep, wide, 128), F32),) * (ITERS + 1)
+        + (pltpu.VMEM((2, 128, 128), F32), pltpu.VMEM((8, 128), F32)),
         in_specs=[hbm] * 4,
-        out_specs=(hbm, hbm),
-        scratch_shapes=[pltpu.VMEM((deep, wide, 128), F32)] * (ITERS + 1)
-        + [
-            pltpu.VMEM((2, 128, 128), F32),
-            pltpu.VMEM((2, members, rows + 8, columns), F32),
-            pltpu.SemaphoreType.DMA((2, 2, groups)),
+        out_specs=(vmem,) * (ITERS + 3),
+        scratch_shapes=[
             pltpu.VMEM((deep, wide, 128), F32),
             pltpu.VMEM((5, wide, 128), F32),
             pltpu.VMEM((members, rows + 8, columns), F32),
@@ -475,8 +503,10 @@
             pltpu.VMEM((128, 128), F32),
             pltpu.VMEM((2, wide, 128), F32),
             pltpu.VMEM((wide, 128), F32),
-            pltpu.VMEM((4, deep + 1, wide, 128), F32),
+            pltpu.VMEM((5, deep + 3, wide, 128), F32),
             pltpu.VMEM((wide, 128), F32),
+            pltpu.VMEM((5 * 144, 256), jnp.bfloat16),
+            pltpu.VMEM(((deep + 2) // 2, 256, 256), jnp.bfloat16),
             pltpu.VMEM((8, 128), F32),
             pltpu.VMEM((nx, 8, 128), F32),
             pltpu.VMEM((ny, 8, 128), F32),
@@ -485,9 +515,24 @@
             pltpu.SemaphoreType.DMA((6 + nx + ny,)),
         ],
         compiler_params=pltpu.CompilerParams(
-            collective_id=0, has_side_effects=True, vmem_limit_bytes=kernel_vmem
+            collective_id=0, has_side_effects=True, vmem_limit_bytes=GRANT
         ),
-    )(right_side, couplings, center, ocean_mask)
+    )(*inputs)
+
+    def second(*refs):
+        combine_kernel(members, rows, *refs)
+
+    return pl.pallas_call(
+        second,
+        out_shape=(jax.ShapeDtypeStruct(right_side.shape, F32),) * 2,
+        in_specs=[vmem] * (ITERS + 3),
+        out_specs=(hbm, hbm),
+        compiler_params=pltpu.CompilerParams(vmem_limit_bytes=GRANT),
+        scratch_shapes=[
+            pltpu.VMEM((2, members, rows + 8, columns), F32),
+            pltpu.SemaphoreType.DMA((2, 2, groups)),
+        ],
+    )(*basis, scale, sums)
 
 
 def solution(mesh):

time: 51 us -> 39.5 us (0.77)
  Pallas kernels: 46.9 us -> 38.8 us
  local copies, waits for them, and re-layouts: 3.37 us -> 0 us
    pallas_call x1 -> x2, Pallas kernels: 46.9 us -> 38.8 us  [the longest x1 35.3 us: on_device(): pl.pallas_call(first, out_shape=(pltpu.VMEM((deep, wide, 128), F32),) * (...]
    unnamed x4 -> x0, local copies, waits for them, and re-layouts: 3.37 us -> none
where the time goes in v1:
time: 39.5 us; the launch traced here: 39.4 us
  Pallas kernels  38.8 us (98%)
  between operations  0.64 us (2%)
    pallas_call x1, Pallas kernels, on_device(): pl.pallas_call(first, out_shape=(pltpu.VMEM((deep, wide, 128), F32),) * (...  35.3 us
    pallas_call x1, Pallas kernels, on_device(): pl.pallas_call(second, out_shape=(jax.ShapeDtypeStruct(right_side.shape,...  3.42 us

profile of v1, /device:TPU:0, one launch (start us, length us, event | category | flops | bytes accessed | tf_op | source)
XLA Modules:
  0.0 39.4 jit_solution(13210603810237029949)
XLA Ops:
  0.6 35.3 %shard_map.59 = (f32[28,168,128]{2,1,0:T(8,128)S(1)}, f32[28,168,128]{2,1,0:T(8,128)S(1)}, f32[28,168,128]{2,1,0:T(8,128)S(1)}, f32[28,168,128]{2,1,0:T(8,128)S(...) custom-call(f32[32,64,128]{2,1,0:T(8,128)} %refs_0_.1, ...), custom_call_target="tpu_custom_call" | custom-call | tf_op jit(solution)/shard_map/pallas_call | solution.py:486
  36.0 3.4 %shard_map.60 = (f32[32,64,128]{2,1,0:T(8,128)}, f32[32,64,128]{2,1,0:T(8,128)}) custom-call(f32[28,168,128]{2,1,0:T(8,128)S(1)} %get-tuple-element.11.refs_0_, f32[28,168,128]{2,1,0:T(8,128)S(1)} %get-tuple-element.12.refs_1_, f32[28,168,128]{2,1,0:T(8,128)S(1)} %get-tuple-element.13.refs_2_, f32[28,168,128]{2,1,0:T(8,128)S(1)} %get-tuple-element.14.refs_3_, ...), custom_call_target="tpu_custom_call" | custom-call | tf_op jit(solution)/shard_map/pallas_call | solution.py:525

commit v2 on v1

--- a/solution.py
+++ b/solution.py
@@ -23,29 +23,28 @@
 
 
 def prepare(members, rows, top, planes, shifted, inv, links, square, lhs, pick):
-    lanes = iota(1)
+    first, chunk, tiles = PAD - 8, 48, 18
+    lanes = lax.broadcasted_iota(jnp.int32, (chunk, 128), 1)
     seam = lanes == rows + 8
     folded = jnp.logical_and(top, lanes >= rows + 8)
-    tiles = 18
-    first = PAD - 8
-
-    @pl.loop(0, tiles)
-    def _(t):
-        at = pl.ds(pl.multiple_of(first + 8 * t, 8), 8)
-        nxt = pl.ds(first + 8 * t + 1, 8)
+    span = rows + 16
+    factor = 1.0 / ROOT
+
+    def before(v):
+        return pltpu.roll(v, 1, 1)
+
+    def after(v):
+        return pltpu.roll(v, 127, 1)
+
+    for t in range(0, 8 * tiles, chunk):
+        at, nxt = slice(first + t, first + t + chunk), slice(first + t + 1, first + t + 1 + chunk)
         for n, p in enumerate((1, 2)):
             shifted[n, at, :] = jnp.where(folded, planes[p, nxt, :], planes[p, at, :])
 
-    def before(v):
-        return pltpu.roll(v, 1, 1)
-
-    def after(v):
-        return pltpu.roll(v, 127, 1)
-
-    @pl.loop(0, tiles)
+    @pl.loop(0, 8 * tiles // chunk)
     def _(t):
-        at = pl.ds(pl.multiple_of(first + 8 * t, 8), 8)
-        prv = pl.ds(first + 8 * t - 1, 8)
+        at = pl.ds(pl.multiple_of(first + chunk * t, 8), chunk)
+        prv = pl.ds(first + chunk * t - 1, chunk)
         cn, ce, cne = planes[0, at, :], shifted[0, at, :], shifted[1, at, :]
         cew, cnw = shifted[0, prv, :], shifted[1, prv, :]
         diag = planes[3, at, :] + cn + ce + cew + cne + cnw + before(cn + cne + cnw)
@@ -56,19 +55,14 @@
         inv[at, :] = jnp.where(seam, after(recip), recip)
         square[at, :] = root
 
-    span = rows + 16
-    lanes = lax.broadcasted_iota(jnp.int32, (16, 128), 1)
-    seam = lanes == rows + 8
-
-    @pl.loop(0, tiles // 2)
+    @pl.loop(0, 8 * tiles // chunk)
     def _(t):
-        at = pl.ds(pl.multiple_of(first + 16 * t, 8), 16)
-        nxt = pl.ds(first + 16 * t + 1, 16)
+        at = pl.ds(pl.multiple_of(first + chunk * t, 8), chunk)
+        nxt = pl.ds(first + chunk * t + 1, chunk)
         here, east = inv[at, :], inv[nxt, :]
         up, up_east = after(here), after(east)
         here_up = jnp.where(seam, before(here), here)
         east_up = jnp.where(seam, before(east), east)
-        factor = 1.0 / ROOT
         cn, ce, cne = planes[0, at, :] * factor, shifted[0, at, :] * factor, shifted[1, at, :] * factor
         values = (cn * here_up * up, ce * here * east, cne * here_up * up_east, cne * east_up * up, here)
         for n, v in enumerate(values):
@@ -80,7 +74,7 @@
             left = jnp.where(lanes < span, top_part, moved)
             right = jnp.where(lanes < 2 * span - 128, moved, low_part)
             right = jnp.where(lanes < 3 * span - 128, right, 0.0)
-            to = pl.ds(pl.multiple_of(8 * tiles * n + 16 * t, 16), 16)
+            to = pl.ds(pl.multiple_of(8 * tiles * n + chunk * t, 16), chunk)
             lhs[to, 0:128] = left.astype(jnp.bfloat16)
             lhs[to, 128:256] = right.astype(jnp.bfloat16)
 
@@ -187,8 +181,8 @@
 def solve_kernel(members, rows, ny, nx, rhs_hbm, coup_hbm, center_hbm, mask_hbm, *refs):
     basis, (scale_ref, sum_ref) = refs[: ITERS + 1], refs[ITERS + 1 : ITERS + 3]
     (
-        field, planes, rhs, coup, center, mask, coef_out, coef_in, rows_out, rows_in, ext,
-        shifted, inv, links, square, lhs, pick, gram, along_x, along_y, load, send, recv,
+        field, links, planes, rhs, coup, center, mask, coef_out, coef_in, rows_out, rows_in, strip_out, corner_out, corner_in, ext,
+        shifted, inv, square, lhs, pick, gram, along_x, along_y, load, send, recv,
     ) = refs[ITERS + 3 :]
     groups = 128 // members
     sub_rows = rows // groups
@@ -217,6 +211,16 @@
     for step in range(1, ny):
         greet((lax.rem(y + step, ny), x))
 
+    @pl.when(y > 0)
+    def _():
+        greet((y - 1, east))
+        greet((y - 1, west))
+
+    @pl.when(top == 0)
+    def _():
+        greet((y + 1, east))
+        greet((y + 1, west))
+
     def copy(src, dst, n, m, there):
         return pltpu.make_async_remote_copy(
             src_ref=src,
@@ -227,9 +231,44 @@
             device_id_type=pl.DeviceIdType.MESH,
         )
 
+    def corner(base, parts):
+        found = []
+        for e in range(2):
+            plain, folded = x + 2 * e - 1, mirror + 1 - 2 * e
+            to = lax.rem(plain + top * (folded - plain) + nx, nx)
+            k = 1 - e + top * (1 + 2 * e)
+            c = copy(
+                corner_out.at[e, parts], corner_in.at[k, parts], base + e, base + k, (y + 1 - top, to)
+            )
+            found.append((jnp.logical_or(top == 0, to != x), c, e, k))
+        for e in range(2):
+            k = 3 - e
+            there = (jnp.maximum(y - 1, 0), east if e else west)
+            c = copy(
+                corner_out.at[2 + e, parts], corner_in.at[k, parts], base + 2 + e, base + k, there
+            )
+            found.append((y > 0, c, 2 + e, k))
+        return found
+
+    def start_corners(found, parts):
+        for n, (remote, c, e, k) in enumerate(found):
+            pl.when(remote)(c.start)
+            if n < 2:
+
+                @pl.when(jnp.logical_not(remote))
+                def _():
+                    corner_in[k, parts] = corner_out[e, parts]
+
+    def corner_arrivals(found, base, parts):
+        for k in range(4):
+            c = copy(corner_out.at[0, parts], corner_in.at[k, parts], base, base + k, (y, east))
+            pl.when(y > 0 if k < 2 else found[k - 2][0])(c.wait_recv)
+
     lanes, subs = iota(1), iota(0)
     flip_lane = jnp.where(top == 1, 127 - lanes, lanes)
     flip_sub = jnp.where(top == 1, 7 - subs, subs)
+    tiles = (slice(PAD, PAD + 8), slice(PAD + 120, PAD + 128))
+    beyond_tiles = (slice(PAD - 8, PAD), slice(PAD + 128, PAD + 136))
     for c in loads[:3]:
         c.wait()
 
@@ -238,22 +277,41 @@
             return coup[p, at, :]
         return center[at, :] if p == 3 else mask[at, :].astype(F32)
 
+    packs = [jnp.zeros((8, 128), F32)] * 4
+    plane = lax.shift_right_logical(lanes, 3)
+    high_lanes = jnp.where(top == 1, rows + 7 - (lanes & 7), rows + (lanes & 7))
+    low_lanes = 8 + (lanes & 7)
+    ext[0:8, :] = jnp.zeros((8, 128), F32)
+    ext[rows + 8 : 128, :] = jnp.zeros((120 - rows, 128), F32)
     for p in range(5):
         coef_out[0, p] = along(along(own(p, slice(rows - 8, rows)), flip_lane, 1), flip_sub, 0)
         coef_out[1, p] = own(p, slice(0, 8))
+        ext[8 : rows + 8, :] = own(p, slice(0, rows))
+        turned = ext[...].T
+        for e, edge in enumerate((turned[0:8], turned[120:128])):
+            strip_out[e, p] = edge
+            packs[e] = jnp.where(plane == p, along(edge, high_lanes, 1), packs[e])
+            packs[2 + e] = jnp.where(plane == p, along(edge, low_lanes, 1), packs[2 + e])
+    for e in range(4):
+        corner_out[e, 0] = along(packs[e], flip_sub, 0) if e < 2 else packs[e]
     choose(members, rows, pick)
-    pl.semaphore_wait(barrier, nx + ny - 2)
-
+    pl.semaphore_wait(barrier, nx + ny - 2 + 2 * (1 - top) + 2 * jnp.minimum(y, 1))
     coef_up = copy(coef_out.at[0], coef_in.at[top], 0, top, up)
     coef_down = copy(coef_out.at[1], coef_in.at[1], 1, 1, down)
     rows_up = copy(rows_out.at[0], rows_in.at[top], 2, 2 + top, up)
     rows_down = copy(rows_out.at[1], rows_in.at[1], 3, 3, down)
+    first = slice(0, 1)
+    later = slice(1, 3)
+    coef_corners, rows_corners = corner(8, first), corner(12, later)
+    sides = [
+        copy(strip_out.at[0], planes.at[:, PAD + 128 : PAD + 136, :], 4, 4, (y, west)),
+        copy(strip_out.at[1], planes.at[:, PAD - 8 : PAD, :], 5, 5, (y, east)),
+    ]
+    start_corners(coef_corners, first)
     coef_up.start()
-
-    @pl.when(y > 0)
-    def _():
-        coef_down.start()
-
+    pl.when(y > 0)(coef_down.start)
+    for c in sides:
+        c.start()
     flat = rhs.reshape(members * tall, 128)
 
     def column(row, block):
@@ -267,25 +325,40 @@
             at = slice(q * members + 8 * b, q * members + 8 * b + 8)
             rows_out[0, at, :] = along(column(high, b), flip_lane, 1)
             rows_out[1, at, :] = column(q, b)
-    rows_up.start()
-
-    @pl.when(y > 0)
-    def _():
-        rows_down.start()
 
     @pl.loop(0, sub_rows)
     def _(r):
         stack = [column(sub_rows * g + r, b) for g in range(groups) for b in range(blocks)]
         field[r + ITERS, PAD : PAD + 128, :] = jnp.concatenate(stack, axis=0).T
 
+    member = lanes & (members - 1)
+    group = lax.shift_right_logical(lanes, members.bit_length() - 1)
+    for e in range(2):
+        packs = [[jnp.zeros((8, 128), F32)] * 2 for _ in range(2)]
+        for q in range(ITERS):
+            here = group == q % groups
+            v = field[sub_rows + q + top * (ITERS - 1 - 2 * q), tiles[e], :]
+            v = along(v, member + (128 - members), 1)
+            packs[0][q // groups] = jnp.where(here, v, packs[0][q // groups])
+            v = along(field[ITERS + q, tiles[e], :], member, 1)
+            packs[1][q // groups] = jnp.where(here, v, packs[1][q // groups])
+        for n in range(2):
+            corner_out[e, 1 + n] = along(packs[0][n], flip_sub, 0)
+            corner_out[2 + e, 1 + n] = packs[1][n]
+    inner = slice(ITERS, ITERS + sub_rows)
+    more = [
+        copy(field.at[inner, tiles[0], :], field.at[inner, beyond_tiles[1], :], 6, 6, (y, west)),
+        copy(field.at[inner, tiles[1], :], field.at[inner, beyond_tiles[0], :], 7, 7, (y, east)),
+    ]
+    start_corners(rows_corners, later)
+    rows_up.start()
+    pl.when(y > 0)(rows_down.start)
+    for c in more:
+        c.start()
     coef_north = copy(coef_out.at[1], coef_in.at[1], 1, 1, down)
     coef_south = copy(coef_out.at[0], coef_in.at[0], 0, 0, up)
     coef_north.wait_recv()
-
-    @pl.when(y > 0)
-    def _():
-        coef_south.wait_recv()
-
+    pl.when(y > 0)(coef_south.wait_recv)
     for p in range(5):
         beyond = coef_in[1, p]
         moved = pltpu.roll(beyond, 1, 0)
@@ -297,23 +370,27 @@
         ext[0:8, :] = jnp.where(y == 0, 0.0, coef_in[0, p])
         ext[8 : rows + 8, :] = own(p, slice(0, rows))
         ext[rows + 8 : rows + 16, :] = beyond
-        ext[rows + 16 : 128, :] = jnp.zeros((112 - rows, 128), F32)
         planes[p, PAD : PAD + 128, :] = ext[...].T
-
-    def sideways(ref, n):
-        return [
-            copy(ref.at[:, PAD : PAD + 8, :], ref.at[:, PAD + 128 : PAD + 136, :], n, n, (y, west)),
-            copy(ref.at[:, PAD + 120 : PAD + 128, :], ref.at[:, PAD - 8 : PAD, :], n + 1, n + 1, (y, east)),
-        ]
-
-    sides = sideways(planes, 4)
     for c in sides:
-        c.start()
+        c.wait_recv()
+    corner_arrivals(coef_corners, 8, first)
+    for e in range(2):
+        low, high = corner_in[e, 0], corner_in[2 + e, 0]
+        for p in range(5):
+            strip = planes[p, beyond_tiles[e], :]
+            shift = 1 - top if p in (0, 2) else 1
+            idx = jnp.clip(lanes - (rows + 8) - shift, 0, 7) + 8 * p
+            north = along(high, idx, 1)
+            if p in (0, 2):
+                joint = jnp.logical_and(lanes == rows + 8, top == 0)
+                north = jnp.where(joint, pltpu.roll(strip, 1, 1), north)
+            south = jnp.where(y == 0, 0.0, along(low, (lanes & 7) + 8 * p, 1))
+            outside = jnp.logical_and(lanes >= rows + 8, lanes < rows + 16)
+            strip = jnp.where(lanes < 8, south, jnp.where(outside, north, strip))
+            planes[p, beyond_tiles[e], :] = strip
+    prepare(members, rows, y == ny - 1, planes, shifted, inv, links, square, lhs, pick)
     copy(rows_out.at[1], rows_in.at[1], 3, 3, down).wait_recv()
-
-    @pl.when(y > 0)
-    def _():
-        copy(rows_out.at[0], rows_in.at[0], 2, 2, up).wait_recv()
+    pl.when(y > 0)(copy(rows_out.at[0], rows_in.at[0], 2, 2, up).wait_recv)
 
     @pl.loop(0, ITERS)
     def _(q):
@@ -327,9 +404,19 @@
         high += [arrived(1, b) for b in range(blocks)]
         field[q + ITERS + sub_rows, PAD : PAD + 128, :] = jnp.concatenate(high, axis=0).T
 
-    more = sideways(field, 6)
     for c in more:
-        c.start()
+        c.wait_recv()
+    corner_arrivals(rows_corners, 12, later)
+    for e in range(2):
+        for q in range(ITERS):
+            idx = member + members * (q % groups)
+            south = along(corner_in[e, 1 + q // groups], idx, 1)
+            south = jnp.where(y == 0, 0.0, south)
+            v = pltpu.roll(field[sub_rows + q, beyond_tiles[e], :], members, 1)
+            field[q, beyond_tiles[e], :] = jnp.where(group == 0, south, v)
+            north = along(corner_in[2 + e, 1 + q // groups], idx, 1)
+            v = pltpu.roll(field[ITERS + q, beyond_tiles[e], :], 128 - members, 1)
+            field[ITERS + sub_rows + q, beyond_tiles[e], :] = jnp.where(group == groups - 1, north, v)
     coef_up.wait_send()
     rows_up.wait_send()
 
@@ -338,11 +425,10 @@
         coef_down.wait_send()
         rows_down.wait_send()
 
-    for c in sides:
-        c.wait()
-    prepare(members, rows, y == ny - 1, planes, shifted, inv, links, square, lhs, pick)
-    for c in more:
-        c.wait()
+    for c in sides + more:
+        c.wait_send()
+    for remote, c, _, _ in coef_corners + rows_corners:
+        pl.when(remote)(c.wait_send)
     iterate(members, rows, field, inv, links, basis, gram)
 
     def sent(source, dst, n, there):
@@ -350,14 +436,14 @@
         c.start()
         return c
 
-    across = [sent(gram, along_x.at[s], 7 + s, (y, lax.rem(x + s, nx))) for s in range(1, nx)]
+    across = [sent(gram, along_x.at[s], 15 + s, (y, lax.rem(x + s, nx))) for s in range(1, nx)]
     scale_ref[0] = inv[PAD : PAD + 128, :].T
     scale_ref[1] = square[PAD : PAD + 128, :].T
     for c in across:
         c.wait()
     along_x[0] = sum((along_x[s] for s in range(1, nx)), gram[...])
     across = [
-        sent(along_x.at[0], along_y.at[s], 6 + nx + s, (lax.rem(y + s, ny), x)) for s in range(1, ny)
+        sent(along_x.at[0], along_y.at[s], 14 + nx + s, (lax.rem(y + s, ny), x)) for s in range(1, ny)
     ]
     for c in across:
         c.wait()
@@ -468,6 +554,7 @@
     members, rows, columns = right_side.shape
     groups = 128 // members
     sub_rows = rows // groups
+    assert lax.axis_size("gx") > 2 and ITERS <= 2 * groups
     assert columns == 128 and members % 8 == 0 and groups * members == 128
     assert 3 * (rows + 16) <= 256 < 4 * (rows + 16) and 2 * (rows + 16) >= 128 and sub_rows % 16 == 0 and sub_rows >= ITERS
     ny, nx = lax.axis_size("gy"), lax.axis_size("gx")
@@ -491,6 +578,7 @@
         out_specs=(vmem,) * (ITERS + 3),
         scratch_shapes=[
             pltpu.VMEM((deep, wide, 128), F32),
+            pltpu.VMEM((5, deep + 3, wide, 128), F32),
             pltpu.VMEM((5, wide, 128), F32),
             pltpu.VMEM((members, rows + 8, columns), F32),
             pltpu.VMEM((3, rows, columns), F32),
@@ -500,10 +588,12 @@
             pltpu.VMEM((2, 5, 8, columns), F32),
             pltpu.VMEM((2, ITERS * members, columns), F32),
             pltpu.VMEM((2, ITERS * members, columns), F32),
+            pltpu.VMEM((2, 5, 8, 128), F32),
+            pltpu.VMEM((4, 3, 8, 128), F32),
+            pltpu.VMEM((4, 3, 8, 128), F32),
             pltpu.VMEM((128, 128), F32),
             pltpu.VMEM((2, wide, 128), F32),
             pltpu.VMEM((wide, 128), F32),
-            pltpu.VMEM((5, deep + 3, wide, 128), F32),
             pltpu.VMEM((wide, 128), F32),
             pltpu.VMEM((5 * 144, 256), jnp.bfloat16),
             pltpu.VMEM(((deep + 2) // 2, 256, 256), jnp.bfloat16),
@@ -511,8 +601,8 @@
             pltpu.VMEM((nx, 8, 128), F32),
             pltpu.VMEM((ny, 8, 128), F32),
             pltpu.SemaphoreType.DMA((4,)),
-            pltpu.SemaphoreType.DMA((6 + nx + ny,)),
-            pltpu.SemaphoreType.DMA((6 + nx + ny,)),
+            pltpu.SemaphoreType.DMA((14 + nx + ny,)),
+            pltpu.SemaphoreType.DMA((14 + nx + ny,)),
         ],
         compiler_params=pltpu.CompilerParams(
             collective_id=0, has_side_effects=True, vmem_limit_bytes=GRANT

time: 39.5 us -> 33.8 us (0.86)
  Pallas kernels: 38.8 us -> 33 us
    pallas_call x1, Pallas kernels: 35.3 us -> 29.6 us  [on_device(): pl.pallas_call(first, out_shape=(pltpu.VMEM((deep, wide, 128), F32),) * (...]
where the time goes in v2:
time: 33.8 us; the launch traced here: 33.7 us
  Pallas kernels  33 us (98%)
  between operations  0.64 us (2%)
    pallas_call x1, Pallas kernels, on_device(): pl.pallas_call(first, out_shape=(pltpu.VMEM((deep, wide, 128), F32),) * (...  29.6 us
    pallas_call x1, Pallas kernels, on_device(): pl.pallas_call(second, out_shape=(jax.ShapeDtypeStruct(right_side.shape,...  3.42 us

profile of v2, /device:TPU:0, one launch (start us, length us, event | category | flops | bytes accessed | tf_op | source)
XLA Modules:
  0.0 33.7 jit_solution(10945701093106886177)
XLA Ops:
  0.6 29.6 %shard_map.59 = (f32[28,168,128]{2,1,0:T(8,128)S(1)}, f32[28,168,128]{2,1,0:T(8,128)S(1)}, f32[28,168,128]{2,1,0:T(8,128)S(1)}, f32[28,168,128]{2,1,0:T(8,128)S(...) custom-call(f32[32,64,128]{2,1,0:T(8,128)} %refs_0_.1, ...), custom_call_target="tpu_custom_call" | custom-call | tf_op jit(solution)/shard_map/pallas_call | solution.py:573
  30.2 3.4 %shard_map.60 = (f32[32,64,128]{2,1,0:T(8,128)}, f32[32,64,128]{2,1,0:T(8,128)}) custom-call(f32[28,168,128]{2,1,0:T(8,128)S(1)} %get-tuple-element.11.refs_0_, f32[28,168,128]{2,1,0:T(8,128)S(1)} %get-tuple-element.12.refs_1_, f32[28,168,128]{2,1,0:T(8,128)S(1)} %get-tuple-element.13.refs_2_, f32[28,168,128]{2,1,0:T(8,128)S(1)} %get-tuple-element.14.refs_3_, ...), custom_call_target="tpu_custom_call" | custom-call | tf_op jit(solution)/shard_map/pallas_call | solution.py:615

commit v3 on v2

--- a/solution.py
+++ b/solution.py
@@ -78,14 +78,24 @@
             lhs[to, 0:128] = left.astype(jnp.bfloat16)
             lhs[to, 128:256] = right.astype(jnp.bfloat16)
 
-    @pl.loop(0, links.shape[1] // 2)
-    def _(p):
-        found = jnp.dot(lhs[...], pick[p], preferred_element_type=F32)
-        for n in range(5):
-            for h in range(2):
+    def spread(p, planes_from, halves):
+        found = jnp.dot(lhs[8 * tiles * planes_from :, :], pick[p], preferred_element_type=F32)
+        for n in range(planes_from, 5):
+            for h in range(halves):
+                at = 8 * tiles * (n - planes_from)
                 links[n, 2 * p + h, first : first + 8 * tiles, :] = found[
-                    8 * tiles * n : 8 * tiles * (n + 1), 128 * h : 128 * h + 128
+                    at : at + 8 * tiles, 128 * h : 128 * h + 128
                 ]
+
+    pairs = pick.shape[0] - 1
+    together = 2 - pairs % 2
+
+    @pl.loop(0, pairs // together)
+    def _(part):
+        for within in range(together):
+            spread(together * part + within, 0, 2)
+
+    spread(pairs, 4, 1)
 
 
 def choose(members, rows, pick):
@@ -294,7 +304,6 @@
             packs[2 + e] = jnp.where(plane == p, along(edge, low_lanes, 1), packs[2 + e])
     for e in range(4):
         corner_out[e, 0] = along(packs[e], flip_sub, 0) if e < 2 else packs[e]
-    choose(members, rows, pick)
     pl.semaphore_wait(barrier, nx + ny - 2 + 2 * (1 - top) + 2 * jnp.minimum(y, 1))
     coef_up = copy(coef_out.at[0], coef_in.at[top], 0, top, up)
     coef_down = copy(coef_out.at[1], coef_in.at[1], 1, 1, down)
@@ -326,10 +335,12 @@
             rows_out[0, at, :] = along(column(high, b), flip_lane, 1)
             rows_out[1, at, :] = column(q, b)
 
-    @pl.loop(0, sub_rows)
-    def _(r):
-        stack = [column(sub_rows * g + r, b) for g in range(groups) for b in range(blocks)]
-        field[r + ITERS, PAD : PAD + 128, :] = jnp.concatenate(stack, axis=0).T
+    @pl.loop(0, sub_rows // 4)
+    def _(part):
+        for within in range(4):
+            r = 4 * part + within
+            stack = [column(sub_rows * g + r, b) for g in range(groups) for b in range(blocks)]
+            field[r + ITERS, PAD : PAD + 128, :] = jnp.concatenate(stack, axis=0).T
 
     member = lanes & (members - 1)
     group = lax.shift_right_logical(lanes, members.bit_length() - 1)
@@ -351,14 +362,15 @@
         copy(field.at[inner, tiles[1], :], field.at[inner, beyond_tiles[0], :], 7, 7, (y, east)),
     ]
     start_corners(rows_corners, later)
-    rows_up.start()
-    pl.when(y > 0)(rows_down.start)
     for c in more:
         c.start()
+    choose(members, rows, pick)
     coef_north = copy(coef_out.at[1], coef_in.at[1], 1, 1, down)
     coef_south = copy(coef_out.at[0], coef_in.at[0], 0, 0, up)
     coef_north.wait_recv()
     pl.when(y > 0)(coef_south.wait_recv)
+    rows_up.start()
+    pl.when(y > 0)(rows_down.start)
     for p in range(5):
         beyond = coef_in[1, p]
         moved = pltpu.roll(beyond, 1, 0)
@@ -392,17 +404,19 @@
     copy(rows_out.at[1], rows_in.at[1], 3, 3, down).wait_recv()
     pl.when(y > 0)(copy(rows_out.at[0], rows_in.at[0], 2, 2, up).wait_recv)
 
-    @pl.loop(0, ITERS)
-    def _(q):
-        def arrived(side, b):
-            return rows_in[side, pl.ds(pl.multiple_of(q * members, 8) + 8 * b, 8), :]
-
-        low = [jnp.where(y == 0, 0.0, arrived(0, b)) for b in range(blocks)]
-        low += [column(sub_rows * g - ITERS + q, b) for g in range(1, groups) for b in range(blocks)]
-        field[q, PAD : PAD + 128, :] = jnp.concatenate(low, axis=0).T
-        high = [column(sub_rows * g + q, b) for g in range(1, groups) for b in range(blocks)]
-        high += [arrived(1, b) for b in range(blocks)]
-        field[q + ITERS + sub_rows, PAD : PAD + 128, :] = jnp.concatenate(high, axis=0).T
+    def arrived(side, q, b):
+        return rows_in[side, pl.ds(pl.multiple_of(q * members, 8) + 8 * b, 8), :]
+
+    @pl.loop(0, ITERS // 2)
+    def _(part):
+        for within in range(2):
+            q = 2 * part + within
+            low = [jnp.where(y == 0, 0.0, arrived(0, q, b)) for b in range(blocks)]
+            low += [column(sub_rows * g - ITERS + q, b) for g in range(1, groups) for b in range(blocks)]
+            field[q, PAD : PAD + 128, :] = jnp.concatenate(low, axis=0).T
+            high = [column(sub_rows * g + q, b) for g in range(1, groups) for b in range(blocks)]
+            high += [arrived(1, q, b) for b in range(blocks)]
+            field[q + ITERS + sub_rows, PAD : PAD + 128, :] = jnp.concatenate(high, axis=0).T
 
     for c in more:
         c.wait_recv()
@@ -525,8 +539,7 @@
     started = []
     for h in range(2):
 
-        @pl.loop(half * h, half * (h + 1))
-        def _(r):
+        def row(r):
             found = ([], [])
             for t in range(16):
                 at = slice(PAD + 8 * t, PAD + 8 * t + 8)
@@ -542,6 +555,11 @@
                         n = 8 * (g * blocks + b)
                         at = pl.ds((o * members + 8 * b) * tall + row, 8, stride=tall)
                         flat[at, :] = turned[n : n + 8, :] * scale
+
+        @pl.loop(0, half // 4)
+        def _(part):
+            for within in range(4):
+                row(half * h + 4 * part + within)
 
         for c in drain(h):
             c.start()

time: 33.8 us -> 32.6 us (0.964)
  Pallas kernels: 33 us -> 31.8 us
    pallas_call x1, Pallas kernels: 3.42 us -> 2.54 us  [on_device(): pl.pallas_call(second, out_shape=(jax.ShapeDtypeStruct(right_side.shape,...]
where the time goes in v3:
time: 32.6 us; the launch traced here: 32.5 us
  Pallas kernels  31.8 us (98%)
  between operations  0.64 us (2%)
    pallas_call x1, Pallas kernels, on_device(): pl.pallas_call(first, out_shape=(pltpu.VMEM((deep, wide, 128), F32),) * (...  29.3 us
    pallas_call x1, Pallas kernels, on_device(): pl.pallas_call(second, out_shape=(jax.ShapeDtypeStruct(right_side.shape,...  2.54 us

profile of v3, /device:TPU:0, one launch (start us, length us, event | category | flops | bytes accessed | tf_op | source)
XLA Modules:
  0.0 32.5 jit_solution(7753477102943265670)
XLA Ops:
  0.6 29.3 %shard_map.59 = (f32[28,168,128]{2,1,0:T(8,128)S(1)}, f32[28,168,128]{2,1,0:T(8,128)S(1)}, f32[28,168,128]{2,1,0:T(8,128)S(1)}, f32[28,168,128]{2,1,0:T(8,128)S(...) custom-call(f32[32,64,128]{2,1,0:T(8,128)} %refs_0_.1, ...), custom_call_target="tpu_custom_call" | custom-call | tf_op jit(solution)/shard_map/pallas_call | solution.py:591
  29.9 2.5 %shard_map.60 = (f32[32,64,128]{2,1,0:T(8,128)}, f32[32,64,128]{2,1,0:T(8,128)}) custom-call(f32[28,168,128]{2,1,0:T(8,128)S(1)} %get-tuple-element.11.refs_0_, f32[28,168,128]{2,1,0:T(8,128)S(1)} %get-tuple-element.12.refs_1_, f32[28,168,128]{2,1,0:T(8,128)S(1)} %get-tuple-element.13.refs_2_, f32[28,168,128]{2,1,0:T(8,128)S(1)} %get-tuple-element.14.refs_3_, ...), custom_call_target="tpu_custom_call" | custom-call | tf_op jit(solution)/shard_map/pallas_call | solution.py:633

commit v4 on v3

--- a/solution.py
+++ b/solution.py
@@ -10,7 +10,8 @@
 PAD = 16
 VMEM = 67043328
 GRANT = 24 * 1024 * 1024
-PAIRS = [(i, j) for i in range(ITERS) for j in range(i, ITERS + 1)]
+SKEW = [(i, j) for i in range(ITERS) for j in range(i + 1, ITERS)]
+SEAM = 16 + ITERS
 F32 = jnp.float32
 
 
@@ -41,10 +42,9 @@
         for n, p in enumerate((1, 2)):
             shifted[n, at, :] = jnp.where(folded, planes[p, nxt, :], planes[p, at, :])
 
-    @pl.loop(0, 8 * tiles // chunk)
-    def _(t):
-        at = pl.ds(pl.multiple_of(first + chunk * t, 8), chunk)
-        prv = pl.ds(first + chunk * t - 1, chunk)
+    for t in range(0, 8 * tiles, chunk):
+        at = slice(first + t, first + t + chunk)
+        prv = slice(first + t - 1, first + t - 1 + chunk)
         cn, ce, cne = planes[0, at, :], shifted[0, at, :], shifted[1, at, :]
         cew, cnw = shifted[0, prv, :], shifted[1, prv, :]
         diag = planes[3, at, :] + cn + ce + cew + cne + cnw + before(cn + cne + cnw)
@@ -55,10 +55,9 @@
         inv[at, :] = jnp.where(seam, after(recip), recip)
         square[at, :] = root
 
-    @pl.loop(0, 8 * tiles // chunk)
-    def _(t):
-        at = pl.ds(pl.multiple_of(first + chunk * t, 8), chunk)
-        nxt = pl.ds(first + chunk * t + 1, chunk)
+    for t in range(0, 8 * tiles, chunk):
+        at = slice(first + t, first + t + chunk)
+        nxt = slice(first + t + 1, first + t + 1 + chunk)
         here, east = inv[at, :], inv[nxt, :]
         up, up_east = after(here), after(east)
         here_up = jnp.where(seam, before(here), here)
@@ -74,7 +73,7 @@
             left = jnp.where(lanes < span, top_part, moved)
             right = jnp.where(lanes < 2 * span - 128, moved, low_part)
             right = jnp.where(lanes < 3 * span - 128, right, 0.0)
-            to = pl.ds(pl.multiple_of(8 * tiles * n + chunk * t, 16), chunk)
+            to = slice(8 * tiles * n + t, 8 * tiles * n + t + chunk)
             lhs[to, 0:128] = left.astype(jnp.bfloat16)
             lhs[to, 128:256] = right.astype(jnp.bfloat16)
 
@@ -117,62 +116,99 @@
         pick[p] = jnp.where(hit, 1.0, 0.0).astype(jnp.bfloat16)
 
 
-def iterate(members, rows, raw, inv, links, basis, gram_ref):
-    groups = 128 // members
-    sub_rows = rows // groups
-    lanes, subs = iota(1), iota(0)
-    group = lax.shift_right_logical(lanes, members.bit_length() - 1)
-
-    @pl.loop(0, sub_rows + 2 * ITERS)
+def apply(k, links, basis, start, stop, tiles, tile):
+    depth = ITERS - 1 - k
+    here, out = basis[k], basis[k + 1]
+    old = basis[k - 1] if k else None
+
+    @pl.loop(0, tiles)
+    def _(t):
+        x0 = PAD - depth + 8 * tile(t)
+        mid, east, west = pl.ds(x0, 8), pl.ds(x0 + 1, 8), pl.ds(x0 - 1, 8)
+
+        def three(r):
+            return here[r, west, :], here[r, mid, :], here[r, east, :]
+
+        dn, cur = three(start - 1), three(start)
+        north = links[0, start - 1 + (1 if start > SEAM else 0), mid, :]
+        for r in range(start, stop):
+            nxt = three(r + 1)
+            c = r + (1 if r >= SEAM else 0)
+            if r == SEAM:
+                north = links[0, c - 1, mid, :]
+            south, north = north, links[0, c, mid, :]
+            total = (north * nxt[1] + south * dn[1]) + (
+                links[1, c, mid, :] * cur[2] + links[1, c, west, :] * cur[0]
+            )
+            total = total + (links[2, c, mid, :] * nxt[2] + links[2, c - 1, west, :] * dn[0])
+            total = total + (links[3, c, west, :] * nxt[0] + links[3, c - 1, mid, :] * dn[2])
+            if old is not None:
+                total = total - old[r, mid, :]
+            out[r, mid, :] = total
+            dn, cur = cur, nxt
+
+
+def begin(raw, links, basis):
+    @pl.loop(ITERS, SEAM)
     def _(r):
-        c = r + (r >= sub_rows + ITERS).astype(jnp.int32)
-        for t in range(18):
+        for t in range(16):
+            at = slice(PAD + 8 * t, PAD + 8 * t + 8)
+            basis[0][r, at, :] = raw[r, at, :] * links[4, r, at, :]
+
+    apply(0, links, basis, ITERS + 1, SEAM - 1, 15, lambda t: t + 1)
+    apply(1, links, basis, ITERS + 2, SEAM - 2, 14, lambda t: t + 1)
+
+
+def iterate(members, rows, top, raw, links, basis, gram_ref):
+    subs = iota(0)
+    group = lax.shift_right_logical(iota(1), members.bit_length() - 1)
+    for r in range(ITERS, SEAM):
+        for t in (0, 17):
             at = slice(PAD - 8 + 8 * t, PAD + 8 * t)
-            basis[0][r, at, :] = raw[r, at, :] * links[4, c, at, :]
-
-    for k in range(ITERS):
+            basis[0][r, at, :] = raw[r, at, :] * links[4, r, at, :]
+
+    apply(0, links, basis, 1, ITERS + 1, 18, lambda t: t)
+    apply(0, links, basis, SEAM - 1, SEAM + ITERS - 1, 18, lambda t: t)
+    apply(0, links, basis, ITERS + 1, SEAM - 1, 3, lambda t: t + 15 * jnp.minimum(t, 1))
+    apply(1, links, basis, 2, ITERS + 2, 17, lambda t: t)
+    apply(1, links, basis, SEAM - 2, SEAM + ITERS - 2, 17, lambda t: t)
+    apply(1, links, basis, ITERS + 2, SEAM - 2, 3, lambda t: t + 14 * jnp.minimum(t, 1))
+    for k in range(2, ITERS):
         depth = ITERS - 1 - k
-        here, out = basis[k], basis[k + 1]
-        old = basis[k - 1] if k else None
-
-        @pl.loop(0, (128 + 2 * depth + 7) // 8)
-        def _(t):
-            x0 = PAD - depth + 8 * t
-            mid, east, west = pl.ds(x0, 8), pl.ds(x0 + 1, 8), pl.ds(x0 - 1, 8)
-
-            def three(r):
-                return here[r, west, :], here[r, mid, :], here[r, east, :]
-
-            start, stop = ITERS - depth, ITERS + sub_rows + depth
-            dn, cur = three(start - 1), three(start)
-            north = links[0, start - 1, mid, :]
-            for r in range(start, stop):
-                nxt = three(r + 1)
-                c = r + (1 if r >= ITERS + sub_rows else 0)
-                if r == ITERS + sub_rows:
-                    north = links[0, c - 1, mid, :]
-                south, north = north, links[0, c, mid, :]
-                total = (north * nxt[1] + south * dn[1]) + (
-                    links[1, c, mid, :] * cur[2] + links[1, c, west, :] * cur[0]
-                )
-                total = total + (links[2, c, mid, :] * nxt[2] + links[2, c - 1, west, :] * dn[0])
-                total = total + (links[3, c, west, :] * nxt[0] + links[3, c - 1, mid, :] * dn[2])
-                if old is not None:
-                    total = total - old[r, mid, :]
-                out[r, mid, :] = total
-                dn, cur = cur, nxt
+        count = (128 + 2 * depth + 7) // 8
+        apply(k, links, basis, ITERS - depth, SEAM + depth, count, lambda t: t)
 
     def body(r, sums):
         sums = list(sums)
         for t in range(16):
             at = slice(PAD + 8 * t, PAD + 8 * t + 8)
             vs = [basis[k][r + ITERS, at, :] for k in range(ITERS + 1)]
-            for n, (i, j) in enumerate(PAIRS):
-                sums[n] = sums[n] + vs[i] * vs[j]
+            for i in range(ITERS):
+                sums[2 * i] = sums[2 * i] + vs[i] * vs[i]
+                sums[2 * i + 1] = sums[2 * i + 1] + vs[i] * vs[i + 1]
         return tuple(sums)
 
     zero = jnp.zeros((8, 128), F32)
-    sums = lax.fori_loop(0, sub_rows, body, (zero,) * len(PAIRS))
+    sums = lax.fori_loop(0, SEAM - ITERS, body, (zero,) * (2 * ITERS))
+    fold = jnp.logical_and(group == 128 // members - 1, top)
+
+    def across(t, sums):
+        sums = list(sums)
+        for u in range(4):
+            x0 = PAD + 32 * t + 8 * u
+            mid, east, west = pl.ds(x0, 8), pl.ds(x0 + 1, 8), pl.ds(x0 - 1, 8)
+            north, right, left = links[0, SEAM - 1, mid, :], links[2, SEAM - 1, mid, :], links[3, SEAM - 1, west, :]
+            here, over = [], []
+            for k in range(ITERS):
+                w = basis[k]
+                v = north * w[SEAM, mid, :] + right * w[SEAM, east, :] + left * w[SEAM, west, :]
+                over.append(jnp.where(fold, v, 0.0))
+                here.append(w[SEAM - 1, mid, :])
+            for n, (i, j) in enumerate(SKEW):
+                sums[n] = sums[n] + (here[i] * over[j] - here[j] * over[i])
+        return tuple(sums)
+
+    sums = sums + lax.fori_loop(0, 4, across, (zero,) * len(SKEW))
     pack = [zero] * 4
     for n, s in enumerate(sums):
         for step in (1, 2, 4):
@@ -401,6 +437,7 @@
             strip = jnp.where(lanes < 8, south, jnp.where(outside, north, strip))
             planes[p, beyond_tiles[e], :] = strip
     prepare(members, rows, y == ny - 1, planes, shifted, inv, links, square, lhs, pick)
+    begin(field, links, basis)
     copy(rows_out.at[1], rows_in.at[1], 3, 3, down).wait_recv()
     pl.when(y > 0)(copy(rows_out.at[0], rows_in.at[0], 2, 2, up).wait_recv)
 
@@ -413,10 +450,15 @@
             q = 2 * part + within
             low = [jnp.where(y == 0, 0.0, arrived(0, q, b)) for b in range(blocks)]
             low += [column(sub_rows * g - ITERS + q, b) for g in range(1, groups) for b in range(blocks)]
-            field[q, PAD : PAD + 128, :] = jnp.concatenate(low, axis=0).T
+            basis[0][q, PAD : PAD + 128, :] = (
+                jnp.concatenate(low, axis=0).T * links[4, q, PAD : PAD + 128, :]
+            )
             high = [column(sub_rows * g + q, b) for g in range(1, groups) for b in range(blocks)]
             high += [arrived(1, q, b) for b in range(blocks)]
-            field[q + ITERS + sub_rows, PAD : PAD + 128, :] = jnp.concatenate(high, axis=0).T
+            r = q + ITERS + sub_rows
+            basis[0][r, PAD : PAD + 128, :] = (
+                jnp.concatenate(high, axis=0).T * links[4, r + 1, PAD : PAD + 128, :]
+            )
 
     for c in more:
         c.wait_recv()
@@ -427,10 +469,12 @@
             south = along(corner_in[e, 1 + q // groups], idx, 1)
             south = jnp.where(y == 0, 0.0, south)
             v = pltpu.roll(field[sub_rows + q, beyond_tiles[e], :], members, 1)
-            field[q, beyond_tiles[e], :] = jnp.where(group == 0, south, v)
+            v = jnp.where(group == 0, south, v)
+            basis[0][q, beyond_tiles[e], :] = v * links[4, q, beyond_tiles[e], :]
             north = along(corner_in[2 + e, 1 + q // groups], idx, 1)
             v = pltpu.roll(field[ITERS + q, beyond_tiles[e], :], 128 - members, 1)
-            field[ITERS + sub_rows + q, beyond_tiles[e], :] = jnp.where(group == groups - 1, north, v)
+            v, r = jnp.where(group == groups - 1, north, v), ITERS + sub_rows + q
+            basis[0][r, beyond_tiles[e], :] = v * links[4, r + 1, beyond_tiles[e], :]
     coef_up.wait_send()
     rows_up.wait_send()
 
@@ -443,7 +487,7 @@
         c.wait_send()
     for remote, c, _, _ in coef_corners + rows_corners:
         pl.when(remote)(c.wait_send)
-    iterate(members, rows, field, inv, links, basis, gram)
+    iterate(members, rows, y == ny - 1, field, links, basis, gram)
 
     def sent(source, dst, n, there):
         c = copy(source, dst, n, n, there)
@@ -517,9 +561,19 @@
     lanes = iota(1)
     sums = sum_ref[...]
     tiles = [along(sums, (lanes & (members - 1)) + members * j, 1) for j in range(4)]
+    found = [
+        jnp.broadcast_to(tiles[n // 8][n % 8 : n % 8 + 1, :], (8, 128))
+        for n in range(2 * ITERS + len(SKEW))
+    ]
     gram = [[None] * (ITERS + 1) for _ in range(ITERS + 1)]
-    for n, (i, j) in enumerate(PAIRS):
-        gram[i][j] = jnp.broadcast_to(tiles[n // 8][n % 8 : n % 8 + 1, :], (8, 128))
+    for i in range(ITERS):
+        gram[i][i], gram[i][i + 1] = found[2 * i], found[2 * i + 1]
+    skew = dict(zip(SKEW, found[2 * ITERS :]))
+    for gap in range(2, ITERS + 1):
+        for i in range(ITERS + 1 - gap):
+            j = i + gap - 1
+            v = gram[i + 1][j] - gram[i][j - 1] + skew[i, j]
+            gram[i][j + 1] = v + gram[i - 1][j] if i else v
     xs, zs = coefficients(gram)
     flat = stage.reshape(2 * members * tall, 128)
     blocks = members // 8
@@ -574,7 +628,7 @@
     sub_rows = rows // groups
     assert lax.axis_size("gx") > 2 and ITERS <= 2 * groups
     assert columns == 128 and members % 8 == 0 and groups * members == 128
-    assert 3 * (rows + 16) <= 256 < 4 * (rows + 16) and 2 * (rows + 16) >= 128 and sub_rows % 16 == 0 and sub_rows >= ITERS
+    assert 3 * (rows + 16) <= 256 < 4 * (rows + 16) and 2 * (rows + 16) >= 128 and sub_rows == SEAM - ITERS
     ny, nx = lax.axis_size("gy"), lax.axis_size("gx")
     vmem = pl.BlockSpec(memory_space=pltpu.VMEM)
     hbm = pl.BlockSpec(memory_space=pltpu.HBM)

time: 32.6 us -> 31.1 us (0.954)
  Pallas kernels: 31.8 us -> 30.3 us
    pallas_call x1, Pallas kernels: 29.3 us -> 27.7 us  [on_device(): pl.pallas_call(first, out_shape=(pltpu.VMEM((deep, wide, 128), F32),) * (...]
where the time goes in v4:
time: 31.1 us; the launch traced here: 30.9 us
  Pallas kernels  30.3 us (97%)
  between operations  0.64 us (2%)
    pallas_call x1, Pallas kernels, on_device(): pl.pallas_call(first, out_shape=(pltpu.VMEM((deep, wide, 128), F32),) * (...  27.7 us
    pallas_call x1, Pallas kernels, on_device(): pl.pallas_call(second, out_shape=(jax.ShapeDtypeStruct(right_side.shape,...  2.54 us

profile of v4, /device:TPU:0, one launch (start us, length us, event | category | flops | bytes accessed | tf_op | source)
XLA Modules:
  0.0 30.9 jit_solution(12826189535390272741)
XLA Ops:
  0.6 27.7 %shard_map.59 = (f32[28,168,128]{2,1,0:T(8,128)S(1)}, f32[28,168,128]{2,1,0:T(8,128)S(1)}, f32[28,168,128]{2,1,0:T(8,128)S(1)}, f32[28,168,128]{2,1,0:T(8,128)S(...) custom-call(f32[32,64,128]{2,1,0:T(8,128)} %refs_0_.1, ...), custom_call_target="tpu_custom_call" | custom-call | tf_op jit(solution)/shard_map/pallas_call | solution.py:645
  28.4 2.5 %shard_map.60 = (f32[32,64,128]{2,1,0:T(8,128)}, f32[32,64,128]{2,1,0:T(8,128)}) custom-call(f32[28,168,128]{2,1,0:T(8,128)S(1)} %get-tuple-element.11.refs_0_, f32[28,168,128]{2,1,0:T(8,128)S(1)} %get-tuple-element.12.refs_1_, f32[28,168,128]{2,1,0:T(8,128)S(1)} %get-tuple-element.13.refs_2_, f32[28,168,128]{2,1,0:T(8,128)S(1)} %get-tuple-element.14.refs_3_, ...), custom_call_target="tpu_custom_call" | custom-call | tf_op jit(solution)/shard_map/pallas_call | solution.py:687

commit v5 on v4

--- a/solution.py
+++ b/solution.py
@@ -6,7 +6,7 @@
 from jax.sharding import PartitionSpec as P
 
 ITERS = 6
-ROOT = 0.28
+ROOT = 0.18
 PAD = 16
 VMEM = 67043328
 GRANT = 24 * 1024 * 1024
@@ -116,7 +116,7 @@
         pick[p] = jnp.where(hit, 1.0, 0.0).astype(jnp.bfloat16)
 
 
-def apply(k, links, basis, start, stop, tiles, tile):
+def apply(k, links, basis, parts, tiles, tile):
     depth = ITERS - 1 - k
     here, out = basis[k], basis[k + 1]
     old = basis[k - 1] if k else None
@@ -129,23 +129,23 @@
         def three(r):
             return here[r, west, :], here[r, mid, :], here[r, east, :]
 
-        dn, cur = three(start - 1), three(start)
-        north = links[0, start - 1 + (1 if start > SEAM else 0), mid, :]
-        for r in range(start, stop):
-            nxt = three(r + 1)
-            c = r + (1 if r >= SEAM else 0)
-            if r == SEAM:
-                north = links[0, c - 1, mid, :]
-            south, north = north, links[0, c, mid, :]
-            total = (north * nxt[1] + south * dn[1]) + (
-                links[1, c, mid, :] * cur[2] + links[1, c, west, :] * cur[0]
-            )
-            total = total + (links[2, c, mid, :] * nxt[2] + links[2, c - 1, west, :] * dn[0])
-            total = total + (links[3, c, west, :] * nxt[0] + links[3, c - 1, mid, :] * dn[2])
-            if old is not None:
-                total = total - old[r, mid, :]
-            out[r, mid, :] = total
-            dn, cur = cur, nxt
+        for start, stop in parts:
+            dn, cur = three(start - 1), three(start)
+            north = links[0, start - 1 + (1 if start > SEAM else 0), mid, :]
+            for r in range(start, stop):
+                nxt = three(r + 1)
+                c = r + (1 if r >= SEAM else 0)
+                if r == SEAM:
+                    north = links[0, c - 1, mid, :]
+                south, north = north, links[0, c, mid, :]
+                total = (north * nxt[1] + south * dn[1]) + (
+                    links[1, c, mid, :] * cur[2] + links[1, c, west, :] * cur[0]
+                )
+                total = total + (links[2, c, mid, :] * nxt[2] + links[2, c - 1, west, :] * dn[0])
+                total = total + (links[3, c, west, :] * nxt[0] + links[3, c - 1, mid, :] * dn[2])
+                total = total - (cur[1] if old is None else cur[1] + old[r, mid, :])
+                out[r, mid, :] = total
+                dn, cur = cur, nxt
 
 
 def begin(raw, links, basis):
@@ -155,8 +155,8 @@
             at = slice(PAD + 8 * t, PAD + 8 * t + 8)
             basis[0][r, at, :] = raw[r, at, :] * links[4, r, at, :]
 
-    apply(0, links, basis, ITERS + 1, SEAM - 1, 15, lambda t: t + 1)
-    apply(1, links, basis, ITERS + 2, SEAM - 2, 14, lambda t: t + 1)
+    apply(0, links, basis, [(ITERS + 1, SEAM - 1)], 15, lambda t: t + 1)
+    apply(1, links, basis, [(ITERS + 2, SEAM - 2)], 14, lambda t: t + 1)
 
 
 def iterate(members, rows, top, raw, links, basis, gram_ref):
@@ -167,16 +167,14 @@
             at = slice(PAD - 8 + 8 * t, PAD + 8 * t)
             basis[0][r, at, :] = raw[r, at, :] * links[4, r, at, :]
 
-    apply(0, links, basis, 1, ITERS + 1, 18, lambda t: t)
-    apply(0, links, basis, SEAM - 1, SEAM + ITERS - 1, 18, lambda t: t)
-    apply(0, links, basis, ITERS + 1, SEAM - 1, 3, lambda t: t + 15 * jnp.minimum(t, 1))
-    apply(1, links, basis, 2, ITERS + 2, 17, lambda t: t)
-    apply(1, links, basis, SEAM - 2, SEAM + ITERS - 2, 17, lambda t: t)
-    apply(1, links, basis, ITERS + 2, SEAM - 2, 3, lambda t: t + 14 * jnp.minimum(t, 1))
+    apply(0, links, basis, [(1, ITERS + 1), (SEAM - 1, SEAM + ITERS - 1)], 18, lambda t: t)
+    apply(0, links, basis, [(ITERS + 1, SEAM - 1)], 3, lambda t: t + 15 * jnp.minimum(t, 1))
+    apply(1, links, basis, [(2, ITERS + 2), (SEAM - 2, SEAM + ITERS - 2)], 17, lambda t: t)
+    apply(1, links, basis, [(ITERS + 2, SEAM - 2)], 3, lambda t: t + 14 * jnp.minimum(t, 1))
     for k in range(2, ITERS):
         depth = ITERS - 1 - k
         count = (128 + 2 * depth + 7) // 8
-        apply(k, links, basis, ITERS - depth, SEAM + depth, count, lambda t: t)
+        apply(k, links, basis, [(ITERS - depth, SEAM + depth)], count, lambda t: t)
 
     def body(r, sums):
         sums = list(sums)
@@ -517,7 +515,7 @@
         for k in range(ITERS + 1):
             terms = []
             if k < len(p):
-                terms.append(p[k])
+                terms.append((1.0 - ROOT) * p[k])
             if 0 < k <= len(p):
                 terms.append(-ROOT * p[k - 1])
             if k + 1 < len(p):

time: 31.1 us -> 31 us (level)
  no operation moved by 1% of the time
where the time goes in v5:
time: 31 us; the launch traced here: 30.9 us
  Pallas kernels  30.3 us (98%)
  between operations  0.64 us (2%)
    pallas_call x1, Pallas kernels, on_device(): pl.pallas_call(first, out_shape=(pltpu.VMEM((deep, wide, 128), F32),) * (...  27.7 us
    pallas_call x1, Pallas kernels, on_device(): pl.pallas_call(second, out_shape=(jax.ShapeDtypeStruct(right_side.shape,...  2.54 us

profile of v5, /device:TPU:0, one launch (start us, length us, event | category | flops | bytes accessed | tf_op | source)
XLA Modules:
  0.0 30.9 jit_solution(9055926950067675651)
XLA Ops:
  0.6 27.7 %shard_map.59 = (f32[28,168,128]{2,1,0:T(8,128)S(1)}, f32[28,168,128]{2,1,0:T(8,128)S(1)}, f32[28,168,128]{2,1,0:T(8,128)S(1)}, f32[28,168,128]{2,1,0:T(8,128)S(...) custom-call(f32[32,64,128]{2,1,0:T(8,128)} %refs_0_.1, ...), custom_call_target="tpu_custom_call" | custom-call | tf_op jit(solution)/shard_map/pallas_call | solution.py:643
  28.4 2.5 %shard_map.60 = (f32[32,64,128]{2,1,0:T(8,128)}, f32[32,64,128]{2,1,0:T(8,128)}) custom-call(f32[28,168,128]{2,1,0:T(8,128)S(1)} %get-tuple-element.11.refs_0_, f32[28,168,128]{2,1,0:T(8,128)S(1)} %get-tuple-element.12.refs_1_, f32[28,168,128]{2,1,0:T(8,128)S(1)} %get-tuple-element.13.refs_2_, f32[28,168,128]{2,1,0:T(8,128)S(1)} %get-tuple-element.14.refs_3_, ...), custom_call_target="tpu_custom_call" | custom-call | tf_op jit(solution)/shard_map/pallas_call | solution.py:685

commit v6 on v5

--- a/solution.py
+++ b/solution.py
@@ -171,24 +171,36 @@
     apply(0, links, basis, [(ITERS + 1, SEAM - 1)], 3, lambda t: t + 15 * jnp.minimum(t, 1))
     apply(1, links, basis, [(2, ITERS + 2), (SEAM - 2, SEAM + ITERS - 2)], 17, lambda t: t)
     apply(1, links, basis, [(ITERS + 2, SEAM - 2)], 3, lambda t: t + 14 * jnp.minimum(t, 1))
-    for k in range(2, ITERS):
+    for k in range(2, ITERS - 1):
         depth = ITERS - 1 - k
         count = (128 + 2 * depth + 7) // 8
         apply(k, links, basis, [(ITERS - depth, SEAM + depth)], count, lambda t: t)
 
+    zero = jnp.zeros((8, 128), F32)
+    fold = jnp.logical_and(group == 128 // members - 1, top)
+    newest = basis[ITERS - 1]
+
     def body(r, sums):
         sums = list(sums)
+        r = r + ITERS
+        share = jnp.where(jnp.logical_and(fold, r == SEAM - 1), 0.5, 1.0)
         for t in range(16):
             at = slice(PAD + 8 * t, PAD + 8 * t + 8)
-            vs = [basis[k][r + ITERS, at, :] for k in range(ITERS + 1)]
+            east, west = (slice(PAD + 8 * t + d, PAD + 8 * t + d + 8) for d in (1, -1))
+            vs = [basis[k][r, at, :] for k in range(ITERS)]
             for i in range(ITERS):
                 sums[2 * i] = sums[2 * i] + vs[i] * vs[i]
-                sums[2 * i + 1] = sums[2 * i + 1] + vs[i] * vs[i + 1]
+                if i + 1 < ITERS:
+                    sums[2 * i + 1] = sums[2 * i + 1] + vs[i] * vs[i + 1]
+            ahead = links[0, r, at, :] * newest[r + 1, at, :]
+            ahead = ahead + links[2, r, at, :] * newest[r + 1, east, :]
+            ahead = ahead + links[3, r, west, :] * newest[r + 1, west, :]
+            ahead = ahead * share + links[1, r, at, :] * newest[r, east, :]
+            sums[-1] = sums[-1] + vs[-1] * ahead
         return tuple(sums)
 
-    zero = jnp.zeros((8, 128), F32)
     sums = lax.fori_loop(0, SEAM - ITERS, body, (zero,) * (2 * ITERS))
-    fold = jnp.logical_and(group == 128 // members - 1, top)
+    sums = sums[:-1] + (sums[-1] + sums[-1],)
 
     def across(t, sums):
         sums = list(sums)
@@ -440,12 +452,10 @@
     pl.when(y > 0)(copy(rows_out.at[0], rows_in.at[0], 2, 2, up).wait_recv)
 
     def arrived(side, q, b):
-        return rows_in[side, pl.ds(pl.multiple_of(q * members, 8) + 8 * b, 8), :]
-
-    @pl.loop(0, ITERS // 2)
-    def _(part):
-        for within in range(2):
-            q = 2 * part + within
+        return rows_in[side, q * members + 8 * b : q * members + 8 * b + 8, :]
+
+    for _ in range(1):
+        for q in range(ITERS):
             low = [jnp.where(y == 0, 0.0, arrived(0, q, b)) for b in range(blocks)]
             low += [column(sub_rows * g - ITERS + q, b) for g in range(1, groups) for b in range(blocks)]
             basis[0][q, PAD : PAD + 128, :] = (
@@ -493,6 +503,7 @@
         return c
 
     across = [sent(gram, along_x.at[s], 15 + s, (y, lax.rem(x + s, nx))) for s in range(1, nx)]
+    apply(ITERS - 1, links, basis, [(ITERS, SEAM)], 16, lambda t: t)
     scale_ref[0] = inv[PAD : PAD + 128, :].T
     scale_ref[1] = square[PAD : PAD + 128, :].T
     for c in across:
@@ -566,6 +577,8 @@
     gram = [[None] * (ITERS + 1) for _ in range(ITERS + 1)]
     for i in range(ITERS):
         gram[i][i], gram[i][i + 1] = found[2 * i], found[2 * i + 1]
+    last = ITERS - 1
+    gram[last][ITERS] = gram[last][ITERS] - gram[last][last] - gram[last - 1][last]
     skew = dict(zip(SKEW, found[2 * ITERS :]))
     for gap in range(2, ITERS + 1):
         for i in range(ITERS + 1 - gap):

time: 31 us -> 30.5 us (0.984)
  Pallas kernels: 30.3 us -> 29.7 us
    pallas_call x1, Pallas kernels: 27.7 us -> 27.2 us  [on_device(): pl.pallas_call(first, out_shape=(pltpu.VMEM((deep, wide, 128), F32),) * (...]
where the time goes in v6:
time: 30.5 us; the launch traced here: 30.4 us
  Pallas kernels  29.7 us (97%)
  between operations  0.64 us (2%)
    pallas_call x1, Pallas kernels, on_device(): pl.pallas_call(first, out_shape=(pltpu.VMEM((deep, wide, 128), F32),) * (...  27.2 us
    pallas_call x1, Pallas kernels, on_device(): pl.pallas_call(second, out_shape=(jax.ShapeDtypeStruct(right_side.shape,...  2.54 us

profile of v6, /device:TPU:0, one launch (start us, length us, event | category | flops | bytes accessed | tf_op | source)
XLA Modules:
  0.0 30.4 jit_solution(6331355241929534467)
XLA Ops:
  0.6 27.2 %shard_map.59 = (f32[28,168,128]{2,1,0:T(8,128)S(1)}, f32[28,168,128]{2,1,0:T(8,128)S(1)}, f32[28,168,128]{2,1,0:T(8,128)S(1)}, f32[28,168,128]{2,1,0:T(8,128)S(...) custom-call(f32[32,64,128]{2,1,0:T(8,128)} %refs_0_.1, ...), custom_call_target="tpu_custom_call" | custom-call | tf_op jit(solution)/shard_map/pallas_call | solution.py:656
  27.8 2.5 %shard_map.60 = (f32[32,64,128]{2,1,0:T(8,128)}, f32[32,64,128]{2,1,0:T(8,128)}) custom-call(f32[28,168,128]{2,1,0:T(8,128)S(1)} %get-tuple-element.11.refs_0_, f32[28,168,128]{2,1,0:T(8,128)S(1)} %get-tuple-element.12.refs_1_, f32[28,168,128]{2,1,0:T(8,128)S(1)} %get-tuple-element.13.refs_2_, f32[28,168,128]{2,1,0:T(8,128)S(1)} %get-tuple-element.14.refs_3_, ...), custom_call_target="tpu_custom_call" | custom-call | tf_op jit(solution)/shard_map/pallas_call | solution.py:698

commit v7 on v6

--- a/solution.py
+++ b/solution.py
@@ -116,14 +116,13 @@
         pick[p] = jnp.where(hit, 1.0, 0.0).astype(jnp.bfloat16)
 
 
-def apply(k, links, basis, parts, tiles, tile):
+def apply(k, links, basis, parts, low, count):
     depth = ITERS - 1 - k
     here, out = basis[k], basis[k + 1]
     old = basis[k - 1] if k else None
 
-    @pl.loop(0, tiles)
-    def _(t):
-        x0 = PAD - depth + 8 * tile(t)
+    def column(t):
+        x0 = PAD - depth + 8 * t
         mid, east, west = pl.ds(x0, 8), pl.ds(x0 + 1, 8), pl.ds(x0 - 1, 8)
 
         def three(r):
@@ -147,6 +146,16 @@
                 out[r, mid, :] = total
                 dn, cur = cur, nxt
 
+    if count > 3:
+
+        @pl.loop(0, count // 2)
+        def _(t):
+            column(low + 2 * t)
+            column(low + 2 * t + 1)
+
+    for t in range(count - count % 2 if count > 3 else 0, count):
+        column(low + t)
+
 
 def begin(raw, links, basis):
     @pl.loop(ITERS, SEAM)
@@ -155,8 +164,8 @@
             at = slice(PAD + 8 * t, PAD + 8 * t + 8)
             basis[0][r, at, :] = raw[r, at, :] * links[4, r, at, :]
 
-    apply(0, links, basis, [(ITERS + 1, SEAM - 1)], 15, lambda t: t + 1)
-    apply(1, links, basis, [(ITERS + 2, SEAM - 2)], 14, lambda t: t + 1)
+    apply(0, links, basis, [(ITERS + 1, SEAM - 1)], 1, 15)
+    apply(1, links, basis, [(ITERS + 2, SEAM - 2)], 1, 14)
 
 
 def iterate(members, rows, top, raw, links, basis, gram_ref):
@@ -167,14 +176,16 @@
             at = slice(PAD - 8 + 8 * t, PAD + 8 * t)
             basis[0][r, at, :] = raw[r, at, :] * links[4, r, at, :]
 
-    apply(0, links, basis, [(1, ITERS + 1), (SEAM - 1, SEAM + ITERS - 1)], 18, lambda t: t)
-    apply(0, links, basis, [(ITERS + 1, SEAM - 1)], 3, lambda t: t + 15 * jnp.minimum(t, 1))
-    apply(1, links, basis, [(2, ITERS + 2), (SEAM - 2, SEAM + ITERS - 2)], 17, lambda t: t)
-    apply(1, links, basis, [(ITERS + 2, SEAM - 2)], 3, lambda t: t + 14 * jnp.minimum(t, 1))
+    apply(0, links, basis, [(1, ITERS + 1), (SEAM - 1, SEAM + ITERS - 1)], 0, 18)
+    apply(0, links, basis, [(ITERS + 1, SEAM - 1)], 0, 1)
+    apply(0, links, basis, [(ITERS + 1, SEAM - 1)], 16, 2)
+    apply(1, links, basis, [(2, ITERS + 2), (SEAM - 2, SEAM + ITERS - 2)], 0, 17)
+    apply(1, links, basis, [(ITERS + 2, SEAM - 2)], 0, 1)
+    apply(1, links, basis, [(ITERS + 2, SEAM - 2)], 15, 2)
     for k in range(2, ITERS - 1):
         depth = ITERS - 1 - k
         count = (128 + 2 * depth + 7) // 8
-        apply(k, links, basis, [(ITERS - depth, SEAM + depth)], count, lambda t: t)
+        apply(k, links, basis, [(ITERS - depth, SEAM + depth)], 0, count)
 
     zero = jnp.zeros((8, 128), F32)
     fold = jnp.logical_and(group == 128 // members - 1, top)
@@ -503,7 +514,7 @@
         return c
 
     across = [sent(gram, along_x.at[s], 15 + s, (y, lax.rem(x + s, nx))) for s in range(1, nx)]
-    apply(ITERS - 1, links, basis, [(ITERS, SEAM)], 16, lambda t: t)
+    apply(ITERS - 1, links, basis, [(ITERS, SEAM)], 0, 16)
     scale_ref[0] = inv[PAD : PAD + 128, :].T
     scale_ref[1] = square[PAD : PAD + 128, :].T
     for c in across:
@@ -591,28 +602,26 @@
     half = sub_rows // 2
     outs = (x_out, r_out)
 
-    def drain(h):
+    def drain(h, o):
         copies = []
-        for o in range(2):
-            for g in range(groups):
-                at = slice(sub_rows * g + half * h, sub_rows * g + half * (h + 1))
-                copies.append(
-                    pltpu.make_async_copy(stage.at[o, :, at, :], outs[o].at[:, at, :], sems.at[h, o, g])
-                )
+        for g in range(groups):
+            at = slice(sub_rows * g + half * h, sub_rows * g + half * (h + 1))
+            copies.append(
+                pltpu.make_async_copy(stage.at[o, :, at, :], outs[o].at[:, at, :], sems.at[h, o, g])
+            )
         return copies
 
     started = []
     for h in range(2):
-
-        def row(r):
-            found = ([], [])
-            for t in range(16):
-                at = slice(PAD + 8 * t, PAD + 8 * t + 8)
-                vs = [basis[k][r + ITERS, at, :] for k in range(ITERS + 1)]
-                found[0].append(sum((xs[k] * vs[k] for k in range(1, ITERS)), xs[0] * vs[0]))
-                found[1].append(sum((zs[k] * vs[k] for k in range(1, ITERS + 1)), zs[0] * vs[0]))
-            for o in range(2):
-                turned = jnp.concatenate(found[o], axis=0).T
+        for o, weights in enumerate((xs, zs)):
+
+            def row(r):
+                found = []
+                for t in range(16):
+                    at = slice(PAD + 8 * t, PAD + 8 * t + 8)
+                    terms = [w * basis[k][r + ITERS, at, :] for k, w in enumerate(weights)]
+                    found.append(sum(terms[1:], terms[0]))
+                turned = jnp.concatenate(found, axis=0).T
                 for g in range(groups):
                     row = sub_rows * g + r
                     scale = jnp.broadcast_to(scale_ref[o, pl.ds(row + 8, 1), :], (8, 128))
@@ -621,14 +630,12 @@
                         at = pl.ds((o * members + 8 * b) * tall + row, 8, stride=tall)
                         flat[at, :] = turned[n : n + 8, :] * scale
 
-        @pl.loop(0, half // 4)
-        def _(part):
-            for within in range(4):
-                row(half * h + 4 * part + within)
-
-        for c in drain(h):
-            c.start()
-            started.append(c)
+            for within in range(half):
+                row(half * h + within)
+
+            for c in drain(h, o):
+                c.start()
+                started.append(c)
     for c in started:
         c.wait()
 

time: 30.5 us -> 29.7 us (0.974)
  Pallas kernels: 29.7 us -> 28.9 us
    pallas_call x1, Pallas kernels: 27.2 us -> 26.7 us  [on_device(): pl.pallas_call(first, out_shape=(pltpu.VMEM((deep, wide, 128), F32),) * (...]
    pallas_call x1, Pallas kernels: 2.54 us -> 2.17 us  [on_device(): pl.pallas_call(second, out_shape=(jax.ShapeDtypeStruct(right_side.shape,...]
where the time goes in v7:
time: 29.7 us; the launch traced here: 29.5 us
  Pallas kernels  28.9 us (97%)
  between operations  0.64 us (2%)
    pallas_call x1, Pallas kernels, on_device(): pl.pallas_call(first, out_shape=(pltpu.VMEM((deep, wide, 128), F32),) * (...  26.7 us
    pallas_call x1, Pallas kernels, on_device(): pl.pallas_call(second, out_shape=(jax.ShapeDtypeStruct(right_side.shape,...  2.17 us

profile of v7, /device:TPU:0, one launch (start us, length us, event | category | flops | bytes accessed | tf_op | source)
XLA Modules:
  0.0 29.5 jit_solution(3746855066781920639)
XLA Ops:
  0.6 26.7 %shard_map.59 = (f32[28,168,128]{2,1,0:T(8,128)S(1)}, f32[28,168,128]{2,1,0:T(8,128)S(1)}, f32[28,168,128]{2,1,0:T(8,128)S(1)}, f32[28,168,128]{2,1,0:T(8,128)S(...) custom-call(f32[32,64,128]{2,1,0:T(8,128)} %refs_0_.1, ...), custom_call_target="tpu_custom_call" | custom-call | tf_op jit(solution)/shard_map/pallas_call | solution.py:663
  27.4 2.2 %shard_map.60 = (f32[32,64,128]{2,1,0:T(8,128)}, f32[32,64,128]{2,1,0:T(8,128)}) custom-call(f32[28,168,128]{2,1,0:T(8,128)S(1)} %get-tuple-element.11.refs_0_, f32[28,168,128]{2,1,0:T(8,128)S(1)} %get-tuple-element.12.refs_1_, f32[28,168,128]{2,1,0:T(8,128)S(1)} %get-tuple-element.13.refs_2_, f32[28,168,128]{2,1,0:T(8,128)S(1)} %get-tuple-element.14.refs_3_, ...), custom_call_target="tpu_custom_call" | custom-call | tf_op jit(solution)/shard_map/pallas_call | solution.py:705

commit v8 on v7

--- a/solution.py
+++ b/solution.py
@@ -215,8 +215,8 @@
 
     def across(t, sums):
         sums = list(sums)
-        for u in range(4):
-            x0 = PAD + 32 * t + 8 * u
+        for u in range(8):
+            x0 = PAD + 64 * t + 8 * u
             mid, east, west = pl.ds(x0, 8), pl.ds(x0 + 1, 8), pl.ds(x0 - 1, 8)
             north, right, left = links[0, SEAM - 1, mid, :], links[2, SEAM - 1, mid, :], links[3, SEAM - 1, west, :]
             here, over = [], []
@@ -229,7 +229,7 @@
                 sums[n] = sums[n] + (here[i] * over[j] - here[j] * over[i])
         return tuple(sums)
 
-    sums = sums + lax.fori_loop(0, 4, across, (zero,) * len(SKEW))
+    sums = sums + lax.fori_loop(0, 2, across, (zero,) * len(SKEW))
     pack = [zero] * 4
     for n, s in enumerate(sums):
         for step in (1, 2, 4):

time: 29.7 us -> 29.7 us (level)
  no operation moved by 1% of the time
where the time goes in v8:
time: 29.7 us; the launch traced here: 29.5 us
  Pallas kernels  28.9 us (97%)
  between operations  0.64 us (2%)
    pallas_call x1, Pallas kernels, on_device(): pl.pallas_call(first, out_shape=(pltpu.VMEM((deep, wide, 128), F32),) * (...  26.7 us
    pallas_call x1, Pallas kernels, on_device(): pl.pallas_call(second, out_shape=(jax.ShapeDtypeStruct(right_side.shape,...  2.17 us

profile of v8, /device:TPU:0, one launch (start us, length us, event | category | flops | bytes accessed | tf_op | source)
XLA Modules:
  0.0 29.5 jit_solution(1666145154581842475)
XLA Ops:
  0.6 26.7 %shard_map.59 = (f32[28,168,128]{2,1,0:T(8,128)S(1)}, f32[28,168,128]{2,1,0:T(8,128)S(1)}, f32[28,168,128]{2,1,0:T(8,128)S(1)}, f32[28,168,128]{2,1,0:T(8,128)S(...) custom-call(f32[32,64,128]{2,1,0:T(8,128)} %refs_0_.1, ...), custom_call_target="tpu_custom_call" | custom-call | tf_op jit(solution)/shard_map/pallas_call | solution.py:663
  27.3 2.2 %shard_map.60 = (f32[32,64,128]{2,1,0:T(8,128)}, f32[32,64,128]{2,1,0:T(8,128)}) custom-call(f32[28,168,128]{2,1,0:T(8,128)S(1)} %get-tuple-element.11.refs_0_, f32[28,168,128]{2,1,0:T(8,128)S(1)} %get-tuple-element.12.refs_1_, f32[28,168,128]{2,1,0:T(8,128)S(1)} %get-tuple-element.13.refs_2_, f32[28,168,128]{2,1,0:T(8,128)S(1)} %get-tuple-element.14.refs_3_, ...), custom_call_target="tpu_custom_call" | custom-call | tf_op jit(solution)/shard_map/pallas_call | solution.py:705
